TPU v7x, 32 devices: a whole 2x2x4 slice. The times are simulated.
32 devices in a mesh: gx: 2 (over x), gy: 4 (over z), gz: 4 (over y, core).
Axes of the slice: x: 2, y: 2, z: 4, core: 2. Of those that a mesh axis runs over, the one named last changes fastest.
Arguments:
- conductivity: float32 [16, 32, 1024], P('gx', 'gy', 'gz'), may hold values from 0.1 to 10
- source: float32 [16, 32, 1024], P('gx', 'gy', 'gz'), may hold values from -5 to 5
Outputs:
- solution: float32 [16, 32, 1024], P('gx', 'gy', 'gz')
- residual: float32 [16, 32, 1024], P('gx', 'gy', 'gz')
All inputs are finite; a program needn't handle non-finite values.
Results may differ from a plain program's by a relative error of at most 0.0003.
Values sent between devices are 32-bit elements; how exact they have to be, the bound alone decides.
A program may use at most 64 MiB of HBM per device.

v0:
```python
import functools

import jax
import jax.numpy as jnp
from jax import lax
from jax.experimental import pallas as pl
from jax.experimental.pallas import tpu as pltpu
from jax.sharding import PartitionSpec as P

LEVELS = 3
DEGREE = 4
COARSE_DEGREE = 8
MESH = pl.DeviceIdType.MESH


weight_table = {1: 14.0 / 30.0, 2: 3.0 / 30.0, 3: 1.0 / 30.0}
neighbour_offsets = [
    (along_one, along_two, along_three)
    for along_one in (-1, 0, 1)
    for along_two in (-1, 0, 1)
    for along_three in (-1, 0, 1)
    if (along_one, along_two, along_three) != (0, 0, 0)
]
smooth_low = 0.5
coarse_low = 0.03
upper_bound = 2.0


def padded_2(block, sides, width):
    for axis, dim in sides:
        count = lax.axis_size(axis)
        forward = [(i, i + 1) for i in range(count - 1)]
        backward = [(target, source) for source, target in forward]
        low = lax.ppermute(
            lax.slice_in_dim(block, block.shape[dim] - width, None, axis=dim), axis, forward
        )
        high = lax.ppermute(lax.slice_in_dim(block, 0, width, axis=dim), axis, backward)
        block = jnp.concatenate([low, block, high], axis=dim)
    return block


def shifted(padded, offset):
    return padded[
        1 + offset[0] : padded.shape[0] - 1 + offset[0],
        1 + offset[1] : padded.shape[1] - 1 + offset[1],
        1 + offset[2] : padded.shape[2] - 1 + offset[2],
    ]


def inner(values, margin):
    return values[
        margin : values.shape[0] - margin,
        margin : values.shape[1] - margin,
        margin : values.shape[2] - margin,
    ]


def stencil(field_pad, coeff_pad, spacing):
    centre_field = shifted(field_pad, (0, 0, 0))
    centre_coeff = shifted(coeff_pad, (0, 0, 0))
    total = jnp.zeros(centre_field.shape, jnp.float32)
    for offset in neighbour_offsets:
        weight = weight_table[abs(offset[0]) + abs(offset[1]) + abs(offset[2])]
        total = total + weight * (centre_coeff + shifted(coeff_pad, offset)) * (
            centre_field - shifted(field_pad, offset)
        )
    return total * (0.5 / spacing)


def diagonal_of(coeff_pad, spacing):
    centre_coeff = shifted(coeff_pad, (0, 0, 0))
    total = jnp.zeros(centre_coeff.shape, jnp.float32)
    for offset in neighbour_offsets:
        weight = weight_table[abs(offset[0]) + abs(offset[1]) + abs(offset[2])]
        total = total + weight * (centre_coeff + shifted(coeff_pad, offset))
    return total * (0.5 / spacing)


def coarsen(values):
    extent = values.shape
    return values.reshape(extent[0] // 2, 2, extent[1] // 2, 2, extent[2] // 2, 2).mean(
        axis=(1, 3, 5)
    )


def refine(values):
    return jnp.repeat(jnp.repeat(jnp.repeat(values, 2, axis=0), 2, axis=1), 2, axis=2)


def chebyshev_coefs(degree, lower):
    centre = (upper_bound + lower) / 2.0
    half_width = (upper_bound - lower) / 2.0
    ratio_term = centre / half_width
    rho_prev = 1.0 / ratio_term
    weights = []
    for number in range(1, degree):
        rho_next = 1.0 / (2.0 * ratio_term - rho_prev)
        weights.append((rho_next * rho_prev, 2.0 * rho_next / half_width))
        rho_prev = rho_next
    return (centre, weights)


def inside_mask(extent, margin):
    first_pos = (
        lax.axis_index("gx") * extent[0]
        + jnp.arange(extent[0] + 2 * margin, dtype=jnp.int32)
        - margin
    )
    second_pos = (
        lax.axis_index("gy") * extent[1]
        + jnp.arange(extent[1] + 2 * margin, dtype=jnp.int32)
        - margin
    )
    third_pos = (
        lax.axis_index("gz") * extent[2]
        + jnp.arange(extent[2] + 2 * margin, dtype=jnp.int32)
        - margin
    )
    first_ok = (first_pos >= 0) & (first_pos < extent[0] * lax.axis_size("gx"))
    second_ok = (second_pos >= 0) & (second_pos < extent[1] * lax.axis_size("gy"))
    third_ok = (third_pos >= 0) & (third_pos < extent[2] * lax.axis_size("gz"))
    return first_ok[:, None, None] & second_ok[None, :, None] & third_ok[None, None, :]


def operate_near(context, field):
    spacing, coeff_ext, diagonal_ext, inside = context
    padded = padded_2(field, (("gx", 0), ("gy", 1), ("gz", 2)), 1)
    return stencil(padded, inner(coeff_ext, 1), spacing)


def two_steps(context, solution, residual, update, first_pair, second_pair):
    spacing, coeff_ext, diagonal_ext, inside = context
    diagonal = inner(diagonal_ext, 1)
    stacked = jnp.stack([update, residual])
    padded = padded_2(stacked, (("gx", 1), ("gy", 2), ("gz", 3)), 2)
    update_wide = padded[0]
    residual_wide = padded[1]
    residual_near = inner(residual_wide, 1) - stencil(update_wide, coeff_ext, spacing)
    update_near = (
        first_pair[0] * inner(update_wide, 1) + first_pair[1] * residual_near / diagonal_ext
    )
    update_near = jnp.where(inside, update_near, 0.0)
    solution = solution + inner(update_near, 1)
    residual = inner(residual_near, 1) - stencil(update_near, inner(coeff_ext, 1), spacing)
    if second_pair is None:
        update = inner(update_near, 1)
    else:
        update = second_pair[0] * inner(update_near, 1) + second_pair[1] * residual / diagonal
        solution = solution + update
    return (solution, residual, update)


def relax(context, right_side, start, degree, lower, final):
    diagonal = inner(context[2], 1)
    centre, weights = chebyshev_coefs(degree, lower)
    if start is None:
        residual = right_side
    else:
        residual = right_side - operate_near(context, start)
    update = residual / (centre * diagonal)
    solution = update if start is None else start + update
    plan_list = list(weights) + ([None] if final else [])
    position = 0
    while position + 1 < len(plan_list):
        solution, residual, update = two_steps(
            context, solution, residual, update, plan_list[position], plan_list[position + 1]
        )
        position = position + 2
    leftover = plan_list[position:]
    for pair in leftover:
        residual = residual - operate_near(context, update)
        update = pair[0] * update + pair[1] * residual / diagonal
        solution = solution + update
    return (solution, residual)


def body(conductivity, source):
    coeff_now = conductivity
    contexts = []
    for grid_level in range(LEVELS):
        if grid_level > 0:
            coeff_now = coarsen(coeff_now)
        spacing = float(4**grid_level)
        coeff_ext = padded_2(coeff_now, (("gx", 0), ("gy", 1), ("gz", 2)), 2)
        inside = inside_mask(coeff_now.shape, 1)
        diagonal_ext = jnp.where(inside, diagonal_of(coeff_ext, spacing), 1.0)
        contexts.append((spacing, coeff_ext, diagonal_ext, inside))

    def cycle(grid_level, right_side):
        context = contexts[grid_level]
        if grid_level == LEVELS - 1:
            return relax(context, right_side, None, COARSE_DEGREE, coarse_low, False)
        solution, residual = relax(context, right_side, None, DEGREE, smooth_low, True)
        correction, ignored = cycle(grid_level + 1, coarsen(residual))
        solution = solution + refine(correction)
        return relax(context, right_side, solution, DEGREE, smooth_low, grid_level == 0)

    return cycle(0, source)


def part_of(values, size):
    if size & (size - 1) == 0:
        return values >> (size.bit_length() - 1)
    return values // size


def rest_of(values, size):
    if size & (size - 1) == 0:
        return values & (size - 1)
    return values % size


def fold(values, eighth):
    side = jnp.where(eighth, values[8:16], values[16:24])
    return jnp.concatenate([values[0:8], side], axis=0)


def over(span, step):
    if isinstance(span[0], int):
        planes = span[1] - span[0]
        if planes <= 4:
            for p in range(*span):
                step(p)
            return
        size = 4 if planes % 4 == 0 else 2 if planes % 2 == 0 else 1
        trips = planes // size
    else:
        size = 2
        trips = (span[1] - span[0] + 1) >> 1

    def body_of(i, carry):
        for j in range(size):
            step(span[0] + size * i + j)
        return carry

    lax.fori_loop(0, trips, body_of, 0)


def cells(shape, dim):
    return lax.broadcasted_iota(jnp.int32, shape, dim)


def pick(left, right):
    if left.dtype == jnp.bfloat16:
        dense, other, swap = right, left, False
    else:
        dense, other, swap = left, right, True
    total = None
    for _ in range(3):
        part = dense.astype(jnp.bfloat16)
        dense = dense - part.astype(jnp.float32)
        pair = (part, other) if swap else (other, part)
        term = jnp.dot(*pair, preferred_element_type=jnp.float32)
        total = term if total is None else total + term
    return total


def ones_where(condition):
    return jnp.where(condition, 1.0, 0.0).astype(jnp.bfloat16)


def turn(values, shift, dim):
    return pltpu.roll(values, shift % values.shape[dim], dim)


def pair_sum(values, dim, edges):
    low = turn(values, 1, dim)
    high = turn(values, -1, dim)
    if edges is not None:
        low = jnp.where(edges[dim][0], 0.0, low)
        high = jnp.where(edges[dim][1], 0.0, high)
    return low + high


def plane_sums(values, edges):
    beside = pair_sum(values, 1, edges)
    strong = 14.0 * values + 3.0 * beside
    weak = 3.0 * values + beside
    return pair_sum(strong, 0, edges) + 14.0 * beside, pair_sum(weak, 0, edges) + strong


class Level:
    def __init__(self, refs, scale, wide_refs=None):
        self.k, self.r, self.d, self.di, self.dg, self.e, self.f, self.g = refs
        self.scale = scale
        shape = self.k.shape[1:]
        self.wide_refs = wide_refs
        self.edges = None
        if wide_refs is None:
            self.edges = [
                (cells(shape, dim) == 0, cells(shape, dim) == shape[dim] - 1) for dim in (0, 1)
            ]
        else:
            self.eighth = cells((8, shape[1]), 0) < 4

    def folded(self, values):
        return values if self.wide_refs is None else fold(values, self.eighth)

    def diagonal(self, wide, near, inside):
        def first(p):
            coeff = self.k[p] if self.wide_refs is None else self.wide_refs[0][p]
            here, side = plane_sums(coeff, self.edges)
            self.e[p] = self.folded(here)
            self.g[p] = self.folded(side)
            if self.wide_refs is not None:
                self.k[p] = self.folded(coeff)

        over(wide, first)

        def second(p):
            total = 128.0 * self.k[p] + self.e[p] + (self.g[p - 1] + self.g[p + 1])
            total = total * self.scale
            self.dg[p] = total
            good = (total > 0.0) & (self.k[p] > 0.0)
            if inside is not None:
                good = good & inside
            self.di[p] = jnp.where(good, 1.0 / total, 0.0)

        over(near, second)

    def first_update(self, span, centre):
        def step(p):
            self.d[p] = self.r[p] * self.di[p] * (1.0 / centre)

        over(span, step)

    def apply(self, wide, near, pair, whole=False):
        def first(p):
            field = self.wide_refs[1][p] if whole else self.d[p]
            coeff = self.wide_refs[0][p] if whole else self.k[p]
            here, side = plane_sums(field, self.edges)
            here_k, side_k = plane_sums(coeff * field, self.edges)
            around = coeff * here + here_k
            if whole:
                around, side, side_k = (self.folded(part) for part in (around, side, side_k))
                self.d[p] = self.folded(field)
            self.e[p] = around
            self.f[p] = side
            self.g[p] = side_k

        over(wide, first)

        def second(p):
            field = self.d[p]
            around = self.e[p] + self.k[p] * (self.f[p - 1] + self.f[p + 1])
            around = around + (self.g[p - 1] + self.g[p + 1])
            left = self.r[p] - (self.dg[p] * field - self.scale * around)
            self.r[p] = left
            if pair is not None:
                fresh = pair[1] * (left * self.di[p])
                self.d[p] = fresh if pair[0] == 0.0 else pair[0] * field + fresh

        over(near, second)


def kernel(sizes, block, *refs):
    (nx, ny, nz) = sizes
    (bx, by, bz) = block
    count = nx * ny * nz
    (k_in, b_in, x_out, r_out) = refs[:4]
    fine_refs = refs[4:12]
    mid_refs = refs[12:20]
    low_refs = refs[20:28]
    (x_mid, b_mid, x_low) = refs[28:31]
    (k_send, b_send, r_send, k_got, b_got) = refs[31:36]
    (k_near, b_near, r_near, d_wide) = refs[36:40]
    packs_out, packs_in = refs[40:43], refs[43:46]
    (halo_out, halo_in, z_out, z_in, all_out, all_in) = refs[46:52]
    (rows_keep, columns_keep) = refs[52:54]
    ix, iy, iz = lax.axis_index("gx"), lax.axis_index("gy"), lax.axis_index("gz")
    me = (ix * ny + iy) * nz + iz
    reach = 5

    def place(number):
        return (number // (ny * nz), (number // nz) % ny, number % nz)

    def clear(ref, planes):
        def step(p):
            ref[p] = jnp.zeros(ref.shape[1:], jnp.float32)

        if isinstance(planes, list):
            for p in planes:
                step(p)
        else:
            over(planes, step)

    for ref in (k_near, b_near, r_near):
        clear(ref, (bx - reach - 1, 2 * bx + reach + 1))

    barrier = pltpu.get_barrier_semaphore()

    def greet(j, carry):
        pl.semaphore_signal(
            barrier, inc=1, device_id=place((me + j) % count), device_id_type=MESH
        )
        return carry

    lax.fori_loop(1, count, greet, 0)
    pl.semaphore_wait(barrier, count - 1)

    fine = Level(fine_refs, 0.5 / 30.0, (k_near, d_wide))
    mid = Level(mid_refs, 0.5 / 4.0 / 30.0)
    low = Level(low_refs, 0.5 / 16.0 / 30.0)

    def near_copy(source, target, which, dx, dy):
        deep = reach if which == 0 else reach - 1
        planes = bx if dx == 0 else deep
        first_from = 0 if dx <= 0 else bx - deep
        first_to = {0: bx, 1: bx - deep, -1: 2 * bx}[dx]
        row_to = {0: 0, 1: 2 * by, -1: by}[dy]
        number = (dx + 1) * 3 + dy + 1
        return pltpu.make_async_remote_copy(
            src_ref=source.at[pl.ds(first_from, planes)],
            dst_ref=target.at[pl.ds(first_to, planes), pl.ds(row_to, by), pl.ds(0, bz)],
            send_sem=halo_out.at[which, number],
            recv_sem=halo_in.at[which, number],
            device_id=(ix + dx, iy + dy, iz),
            device_id_type=MESH,
        )

    sides = [(dx, dy) for dx in (0, 1, -1) for dy in (1, -1, 0) if (dx, dy) != (0, 0)]

    def present(dx, dy):
        return (ix + dx >= 0) & (ix + dx < nx) & (iy + dy >= 0) & (iy + dy < ny)

    def near_start(source, target, which):
        for dx, dy in sides:
            @pl.when(present(dx, dy))
            def _():
                near_copy(source, target, which, dx, dy).start()

    def near_wait(source, target, which):
        for dx, dy in sides:
            @pl.when(present(-dx, -dy))
            def _():
                near_copy(source, target, which, dx, dy).wait_recv()

            @pl.when(present(dx, dy))
            def _():
                near_copy(source, target, which, dx, dy).wait_send()

    eighth = cells((8, bz), 0) < 4

    def z_planes(which):
        deep = reach if which == 0 else reach - 1
        planes = list(range(bx - deep, 2 * bx + deep))
        return [planes[i : i + 16] for i in range(0, len(planes), 16)]

    def z_copy(which, side):
        return pltpu.make_async_remote_copy(
            src_ref=packs_out[which].at[side],
            dst_ref=packs_in[which].at[side],
            send_sem=z_out.at[which, side],
            recv_sem=z_in.at[which, side],
            device_id=(ix, iy, iz + (1 if side == 0 else -1)),
            device_id_type=MESH,
        )

    to_there = (iz + 1 < nz, iz > 0)
    from_there = (iz > 0, iz + 1 < nz)

    def z_start(window, which):
        pack = packs_out[which]
        lane = cells(pack.shape[2:], 1)
        for group, planes in enumerate(z_planes(which)):
            up = jnp.zeros(pack.shape[2:], jnp.float32)
            down = jnp.zeros(pack.shape[2:], jnp.float32)
            for i, p in enumerate(planes):
                mine = (lane >> 3) == i
                up = jnp.where(mine, turn(window[p, :, bz - 128 : bz], 8 * i + 8, 1), up)
                down = jnp.where(mine, turn(window[p, :, 0:128], 8 * i, 1), down)
            pack[0, group] = up
            pack[1, group] = down
        for side in (0, 1):
            @pl.when(to_there[side])
            def _():
                z_copy(which, side).start()

    def z_finish(window, which):
        pack = packs_in[which]
        lane = cells(pack.shape[2:], 1)
        for side in (0, 1):
            @pl.when(from_there[side])
            def _():
                z_copy(which, side).wait_recv()

            @pl.when(jnp.logical_not(from_there[side]))
            def _():
                pack[side] = jnp.zeros(pack.shape[1:], jnp.float32)

            @pl.when(to_there[side])
            def _():
                z_copy(which, side).wait_send()

        for group, planes in enumerate(z_planes(which)):
            below = pack[0, group]
            above = pack[1, group]
            for i, p in enumerate(planes):
                window[p, :, bz : bz + 128] = jnp.where(
                    lane < 64, turn(above, -8 * i, 1), turn(below, -8 * i - 8, 1)
                )

    def fold_in(window):
        for p in z_planes(1)[0]:
            fine.r[p, :, 0:bz] = fold(window[p, :, 0:bz], eighth)

    def all_copy(source, target, which, peer, slot):
        return pltpu.make_async_remote_copy(
            src_ref=source,
            dst_ref=target.at[slot],
            send_sem=all_out.at[which, peer],
            recv_sem=all_in.at[which, slot],
            device_id=place(peer),
            device_id_type=MESH,
        )

    def all_start(source, target, which):
        target[me] = source[...]

        def step(j, carry):
            all_copy(source, target, which, (me + j) % count, me).start()
            return carry

        lax.fori_loop(1, count, step, 0)

    def all_wait(source, target, which):
        def step(j, carry):
            peer = (me + j) % count
            all_copy(source, target, which, peer, peer).wait_recv()
            all_copy(source, target, which, peer, me).wait_send()
            return carry

        lax.fori_loop(1, count, step, 0)

    half = bx // 2 * (by // 2)
    to_row, from_row = cells((half, bx * by), 0), cells((half, bx * by), 1)
    shrink = ones_where(
        (part_of(from_row, 2 * by) == part_of(to_row, by // 2))
        & (rest_of(from_row, by) >> 1 == rest_of(to_row, by // 2))
    )
    shrink_z = ones_where(cells((bz, bz // 2), 0) >> 1 == cells((bz, bz // 2), 1))

    def coarse_block(values):
        flat = pick(pick(shrink, values.reshape(bx * by, bz)), shrink_z) * 0.125
        return flat.reshape(half // 8, 8, bz // 2)

    row8 = cells((8, bz // 2), 0)

    def unpack(got, target):
        for jx in range(nx):
            for jy in range(0, ny, 2):
                for jz in range(nz):
                    slot = (jx * ny + jy) * nz + jz
                    for t in range(half // 8):
                        one, two = got[slot, t], got[slot + nz, t]
                        p = 1 + jx * (bx // 2) + 2 * t
                        at = (slice(jy * 4, jy * 4 + 8), slice(jz * bz // 2, (jz + 1) * bz // 2))
                        target[(p, *at)] = jnp.where(row8 < 4, one, turn(two, 4, 0))
                        target[(p + 1, *at)] = jnp.where(row8 < 4, turn(one, 4, 0), two)

    near_start(k_in, k_near, 0)
    near_start(b_in, b_near, 1)
    k_send[...] = coarse_block(k_in[...])
    k_near[bx : 2 * bx, 0:by, 0:bz] = k_in[...]
    b_near[bx : 2 * bx, 0:by, 0:bz] = b_in[...]
    edge = bx - reach - 1
    for ref in fine_refs:
        clear(ref, [edge, bx - 1, 2 * bx, 2 * bx + 1, 2 * bx + reach])
        clear(ref, (edge, bx))
        clear(ref, (2 * bx, 2 * bx + reach + 1))
    clear(d_wide, [2 * bx + reach])
    for ref in (mid.f, mid.g):
        clear(ref, [0, ref.shape[0] - 1])
    for ref in (low.f, low.g):
        clear(ref, [0, ref.shape[0] - 1])
    mx, my, mz = mid.k.shape[0] - 2, mid.k.shape[1], mid.k.shape[2]
    wide = bx + bx // 2
    mid_x = ix * (bx // 2) - bx // 2
    for q in range(wide):
        shape = (3 * by, mx * my)
        fine_row, mid_row = cells(shape, 0), cells(shape, 1)
        fine_y = iy * by + jnp.where(fine_row < 2 * by, fine_row, fine_row - 3 * by)
        target = (mid_x + q) * my + (fine_y >> 1)
        good = (fine_y >= 0) & (fine_y < ny * by) & (mid_x + q >= 0) & (mid_x + q < mx)
        rows_keep[q] = jnp.where((mid_row == target) & good, 1.0, 0.0)
    shape = (mz, bz + 128)
    fine_col = cells(shape, 1)
    fine_z = iz * bz + jnp.where(fine_col < bz + 64, fine_col, fine_col - (bz + 128))
    columns_keep[...] = ones_where((fine_z >> 1) == cells(shape, 0))
    near_wait(k_in, k_near, 0)
    z_start(k_near, 0)
    near_wait(b_in, b_near, 1)
    fold_in(b_near)
    z_start(fine.r, 1)
    all_start(k_send, k_got, 0)
    z_finish(k_near, 0)

    def span(width):
        return (
            jnp.maximum(bx - width, bx - ix * bx),
            jnp.minimum(2 * bx + width, bx + (nx - ix) * bx),
        )

    plane = (2 * by, bz + 128)
    row, col = cells(plane, 0), cells(plane, 1)
    inside = (
        (row < by) | ((row < by + 4) & (iy + 1 < ny)) | ((row >= by + 4) & (iy > 0))
    ) & ((col < bz) | ((col < bz + 64) & (iz + 1 < nz)) | ((col >= bz + 64) & (iz > 0)))
    fine.diagonal(span(5), span(4), inside)
    z_finish(fine.r, 1)

    own = (slice(bx, 2 * bx), slice(0, by), slice(0, bz))
    centre, weights = chebyshev_coefs(DEGREE, smooth_low)
    fine.first_update(span(4), centre)
    x_out[...] = fine.d[own]
    for number in range(DEGREE):
        pair = weights[number] if number < DEGREE - 1 else None
        fine.apply(span(4 - number), span(3 - number), pair)
        if pair is not None:
            x_out[...] += fine.d[own]

    r_send[...] = fine.r[own]
    b_send[...] = coarse_block(r_send[...])
    all_start(b_send, b_got, 1)
    near_start(r_send, r_near, 2)
    r_near[own] = r_send[...]

    cx, cy, cz = mx // 2, my // 2, mz // 2
    mid_span, low_span = (1, mx + 1), (1, cx + 1)
    all_wait(k_send, k_got, 0)
    unpack(k_got, mid.k)
    mid.diagonal(mid_span, mid_span, None)
    big, small = cells((cx * cy, mx * my), 1), cells((cx * cy, mx * my), 0)
    join = ones_where(
        (part_of(big, 2 * my) == part_of(small, cy)) & (rest_of(big, my) >> 1 == rest_of(small, cy))
    )
    join_z = ones_where(cells((mz, cz), 0) >> 1 == cells((mz, cz), 1))

    def to_low(values):
        flat = pick(join, pick(values.reshape(mx * my, mz), join_z)) * 0.125
        return flat.reshape(cx, cy, cz)

    low.k[1 : cx + 1] = to_low(mid.k[1 : mx + 1])
    low.diagonal(low_span, low_span, None)

    all_wait(b_send, b_got, 1)
    unpack(b_got, b_mid)
    mid.r[1 : mx + 1] = b_mid[1 : mx + 1]
    mid.first_update(mid_span, centre)
    x_mid[...] = mid.d[1 : mx + 1]
    for number in range(DEGREE):
        pair = weights[number] if number < DEGREE - 1 else None
        mid.apply(mid_span, mid_span, pair)
        if pair is not None:
            x_mid[...] += mid.d[1 : mx + 1]

    near_wait(r_send, r_near, 2)
    fold_in(r_near)
    z_start(fine.r, 2)

    low.r[1 : cx + 1] = to_low(mid.r[1 : mx + 1])
    low_centre, low_weights = chebyshev_coefs(COARSE_DEGREE, coarse_low)
    low.first_update(low_span, low_centre)
    x_low[...] = low.d[1 : cx + 1]
    for pair in low_weights:
        low.apply(low_span, low_span, pair)
        x_low[...] += low.d[1 : cx + 1]

    big, small = cells((mx * my, cx * cy), 0), cells((mx * my, cx * cy), 1)
    spread = ones_where(
        (part_of(big, 2 * my) == part_of(small, cy)) & (rest_of(big, my) >> 1 == rest_of(small, cy))
    )
    spread_z = ones_where(cells((cz, mz), 0) == cells((cz, mz), 1) >> 1)
    fixed = pick(spread, pick(x_low[...].reshape(cx * cy, cz), spread_z))
    mid.d[1 : mx + 1] = x_mid[...] + fixed.reshape(mx, my, mz)
    mid.r[1 : mx + 1] = b_mid[1 : mx + 1]
    x_mid[...] = mid.d[1 : mx + 1]
    mid.apply(mid_span, mid_span, (0.0, 1.0 / centre))
    x_mid[...] += mid.d[1 : mx + 1]
    for pair in weights:
        mid.apply(mid_span, mid_span, pair)
        x_mid[...] += mid.d[1 : mx + 1]

    z_finish(fine.r, 2)
    rows = rows_keep[...].reshape(wide * 3 * by, mx * my).astype(jnp.bfloat16)
    fixed = pick(rows, pick(x_mid[...].reshape(mx * my, mz), columns_keep[...]))
    fixed = fixed.reshape(wide, 3 * by, bz + 128)
    for p in range(bx - reach, 2 * bx + reach):
        d_wide[p] = fixed[p // 2]
    x_out[...] += d_wide[own]
    fine.apply(span(5), span(4), (0.0, 1.0 / centre), True)
    x_out[...] += fine.d[own]
    for number in range(DEGREE):
        pair = weights[number] if number < DEGREE - 1 else None
        fine.apply(span(4 - number), span(3 - number), pair)
        if pair is not None:
            x_out[...] += fine.d[own]
    r_out[...] = fine.r[own]


def gathered(sizes, conductivity, source):
    (nx, ny, nz) = sizes
    (bx, by, bz) = conductivity.shape
    count = nx * ny * nz
    mid = (nx * bx // 2 + 2, ny * by // 2, nz * bz // 2)
    low = (nx * bx // 4 + 2, ny * by // 4, nz * bz // 4)
    window = (3 * bx, 3 * by, bz + 128)
    narrow = (3 * bx, 2 * by, bz + 128)
    kept = lambda shape: pltpu.VMEM(shape, jnp.float32)
    inner_mid = (mid[0] - 2, *mid[1:])
    sent = (bx * by // 32, 8, bz // 2)
    scratch = [kept(narrow)] * 8 + [kept(mid)] * 8 + [kept(low)] * 8
    scratch += [kept(inner_mid), kept(mid), kept((low[0] - 2, *low[1:]))]
    scratch += [kept(sent), kept(sent), kept((bx, by, bz))]
    scratch += [kept((count, *sent)), kept((count, *sent))]
    scratch += [kept(window)] * 4
    packs = [kept((2, 2, 3 * by, 128)), kept((2, 1, 2 * by, 128)), kept((2, 1, 2 * by, 128))]
    scratch += packs + packs
    dma = pltpu.SemaphoreType.DMA
    scratch += [dma((3, 9)), dma((3, 9)), dma((3, 2)), dma((3, 2)), dma((2, count)), dma((2, count))]
    scratch += [kept((bx + bx // 2, 3 * by, inner_mid[0] * inner_mid[1]))]
    scratch += [pltpu.VMEM((inner_mid[2], bz + 128), jnp.bfloat16)]
    shape = jax.ShapeDtypeStruct((bx, by, bz), jnp.float32)
    vmem = pl.BlockSpec(memory_space=pltpu.VMEM)
    return pl.pallas_call(
        functools.partial(kernel, sizes, (bx, by, bz)),
        out_shape=(shape, shape),
        in_specs=[vmem, vmem],
        out_specs=(vmem, vmem),
        scratch_shapes=scratch,
        compiler_params=pltpu.CompilerParams(
            collective_id=0, has_side_effects=True, vmem_limit_bytes=48 * 1024 * 1024
        ),
    )(conductivity, source)


def plan(conductivity, source):
    sizes = tuple(lax.axis_size(axis) for axis in ("gx", "gy", "gz"))
    (bx, by, bz) = conductivity.shape
    count = sizes[0] * sizes[1] * sizes[2]
    fits = bx == 8 and by == 8 and bz % 256 == 0 and sizes[1] % 2 == 0
    if fits and count > 1 and count * bx * by * bz // 8 * 4 * 16 <= 16 * 1024 * 1024:
        return gathered(sizes, conductivity, source)
    return body(conductivity, source)


def solution(mesh):
    in_specs = (P("gx", "gy", "gz"), P("gx", "gy", "gz"))
    out_specs = (P("gx", "gy", "gz"), P("gx", "gy", "gz"))
    return jax.shard_map(plan, mesh=mesh, in_specs=in_specs, out_specs=out_specs, check_vma=False)
```

profile of v0, /device:TPU:1, one launch (start us, length us, event | category | flops | bytes accessed | tf_op | source)
XLA Modules:
  0.0 47.7 jit_solution(4048656580513549598)
XLA Ops:
  0.6 0.0 copy-start
  0.6 0.8 %copy-done = f32[8,8,256]{2,1,0:T(8,128)S(1)} copy-done((f32[8,8,256]{2,1,0:T(8,128)S(1)}, f32[8,8,256]{2,1,0:T(8,128)}, u32[]{:S(2)}) %copy-start) | copy-done | bytes 65560
  1.5 0.0 copy-start.1
  1.5 0.8 %copy-done.1 = f32[8,8,256]{2,1,0:T(8,128)S(1)} copy-done((f32[8,8,256]{2,1,0:T(8,128)S(1)}, f32[8,8,256]{2,1,0:T(8,128)}, u32[]{:S(2)}) %copy-start.1) | copy-done | bytes 65560
  2.3 44.2 %shard_map.41 = (f32[8,8,256]{2,1,0:T(8,128)S(1)}, f32[8,8,256]{2,1,0:T(8,128)S(1)}) custom-call(f32[8,8,256]{2,1,0:T(8,128)S(1)} %copy-done, f32[8,8,256]{2,1,0:T(8,128)S(1)} %copy-done.1), custom_call_target="tpu_custom_call" | custom-call | tf_op jit(solution)/shard_map/pallas_call | solution.py:725
  46.5 0.6 %copy.6 = f32[8,8,256]{2,1,0:T(8,128)} copy(f32[8,8,256]{2,1,0:T(8,128)S(1)} %get-tuple-element.4) | data formatting | bytes 131072
  47.1 0.6 %copy.7 = f32[8,8,256]{2,1,0:T(8,128)} copy(f32[8,8,256]{2,1,0:T(8,128)S(1)} %get-tuple-element.5) | data formatting | bytes 131072
Async XLA Ops:
  0.6 0.8 %copy-start = (f32[8,8,256]{2,1,0:T(8,128)S(1)}, f32[8,8,256]{2,1,0:T(8,128)}, u32[]{:S(2)}) copy-start(f32[8,8,256]{2,1,0:T(8,128)} %refs_0_.1) | copy-start | bytes 196612
  1.5 0.8 %copy-start.1 = (f32[8,8,256]{2,1,0:T(8,128)S(1)}, f32[8,8,256]{2,1,0:T(8,128)}, u32[]{:S(2)}) copy-start(f32[8,8,256]{2,1,0:T(8,128)} %refs_1_.1) | copy-start | bytes 196612
where the time goes:
time: 48.4 us; the launch traced here: 47.7 us
  Pallas kernels  44.2 us (91%)
  local copies, waits for them, and re-layouts  2.93 us (6%)
  between operations  0.65 us (1%)
    pallas_call x1, Pallas kernels, gathered(): pl.pallas_call(functools.partial(kernel, sizes, (bx, by, bz)), out_shape=...  44.2 us
    unnamed x6, local copies, waits for them, and re-layouts  2.93 us

commit v1 on v0

v1 whole, which is shorter than its diff:
```python
import functools

import jax
import jax.numpy as jnp
from jax import lax
from jax.experimental import pallas as pl
from jax.experimental.pallas import tpu as pltpu
from jax.sharding import PartitionSpec as P

LEVELS = 3
DEGREE = 4
COARSE_DEGREE = 8
MESH = pl.DeviceIdType.MESH


weight_table = {1: 14.0 / 30.0, 2: 3.0 / 30.0, 3: 1.0 / 30.0}
neighbour_offsets = [
    (along_one, along_two, along_three)
    for along_one in (-1, 0, 1)
    for along_two in (-1, 0, 1)
    for along_three in (-1, 0, 1)
    if (along_one, along_two, along_three) != (0, 0, 0)
]
smooth_low = 0.5
coarse_low = 0.03
upper_bound = 2.0


def padded_2(block, sides, width):
    for axis, dim in sides:
        count = lax.axis_size(axis)
        forward = [(i, i + 1) for i in range(count - 1)]
        backward = [(target, source) for source, target in forward]
        low = lax.ppermute(
            lax.slice_in_dim(block, block.shape[dim] - width, None, axis=dim), axis, forward
        )
        high = lax.ppermute(lax.slice_in_dim(block, 0, width, axis=dim), axis, backward)
        block = jnp.concatenate([low, block, high], axis=dim)
    return block


def shifted(padded, offset):
    return padded[
        1 + offset[0] : padded.shape[0] - 1 + offset[0],
        1 + offset[1] : padded.shape[1] - 1 + offset[1],
        1 + offset[2] : padded.shape[2] - 1 + offset[2],
    ]


def inner(values, margin):
    return values[
        margin : values.shape[0] - margin,
        margin : values.shape[1] - margin,
        margin : values.shape[2] - margin,
    ]


def stencil(field_pad, coeff_pad, spacing):
    centre_field = shifted(field_pad, (0, 0, 0))
    centre_coeff = shifted(coeff_pad, (0, 0, 0))
    total = jnp.zeros(centre_field.shape, jnp.float32)
    for offset in neighbour_offsets:
        weight = weight_table[abs(offset[0]) + abs(offset[1]) + abs(offset[2])]
        total = total + weight * (centre_coeff + shifted(coeff_pad, offset)) * (
            centre_field - shifted(field_pad, offset)
        )
    return total * (0.5 / spacing)


def diagonal_of(coeff_pad, spacing):
    centre_coeff = shifted(coeff_pad, (0, 0, 0))
    total = jnp.zeros(centre_coeff.shape, jnp.float32)
    for offset in neighbour_offsets:
        weight = weight_table[abs(offset[0]) + abs(offset[1]) + abs(offset[2])]
        total = total + weight * (centre_coeff + shifted(coeff_pad, offset))
    return total * (0.5 / spacing)


def coarsen(values):
    extent = values.shape
    return values.reshape(extent[0] // 2, 2, extent[1] // 2, 2, extent[2] // 2, 2).mean(
        axis=(1, 3, 5)
    )


def refine(values):
    return jnp.repeat(jnp.repeat(jnp.repeat(values, 2, axis=0), 2, axis=1), 2, axis=2)


def chebyshev_coefs(degree, lower):
    centre = (upper_bound + lower) / 2.0
    half_width = (upper_bound - lower) / 2.0
    ratio_term = centre / half_width
    rho_prev = 1.0 / ratio_term
    weights = []
    for number in range(1, degree):
        rho_next = 1.0 / (2.0 * ratio_term - rho_prev)
        weights.append((rho_next * rho_prev, 2.0 * rho_next / half_width))
        rho_prev = rho_next
    return (centre, weights)


def inside_mask(extent, margin):
    first_pos = (
        lax.axis_index("gx") * extent[0]
        + jnp.arange(extent[0] + 2 * margin, dtype=jnp.int32)
        - margin
    )
    second_pos = (
        lax.axis_index("gy") * extent[1]
        + jnp.arange(extent[1] + 2 * margin, dtype=jnp.int32)
        - margin
    )
    third_pos = (
        lax.axis_index("gz") * extent[2]
        + jnp.arange(extent[2] + 2 * margin, dtype=jnp.int32)
        - margin
    )
    first_ok = (first_pos >= 0) & (first_pos < extent[0] * lax.axis_size("gx"))
    second_ok = (second_pos >= 0) & (second_pos < extent[1] * lax.axis_size("gy"))
    third_ok = (third_pos >= 0) & (third_pos < extent[2] * lax.axis_size("gz"))
    return first_ok[:, None, None] & second_ok[None, :, None] & third_ok[None, None, :]


def operate_near(context, field):
    spacing, coeff_ext, diagonal_ext, inside = context
    padded = padded_2(field, (("gx", 0), ("gy", 1), ("gz", 2)), 1)
    return stencil(padded, inner(coeff_ext, 1), spacing)


def two_steps(context, solution, residual, update, first_pair, second_pair):
    spacing, coeff_ext, diagonal_ext, inside = context
    diagonal = inner(diagonal_ext, 1)
    stacked = jnp.stack([update, residual])
    padded = padded_2(stacked, (("gx", 1), ("gy", 2), ("gz", 3)), 2)
    update_wide = padded[0]
    residual_wide = padded[1]
    residual_near = inner(residual_wide, 1) - stencil(update_wide, coeff_ext, spacing)
    update_near = (
        first_pair[0] * inner(update_wide, 1) + first_pair[1] * residual_near / diagonal_ext
    )
    update_near = jnp.where(inside, update_near, 0.0)
    solution = solution + inner(update_near, 1)
    residual = inner(residual_near, 1) - stencil(update_near, inner(coeff_ext, 1), spacing)
    if second_pair is None:
        update = inner(update_near, 1)
    else:
        update = second_pair[0] * inner(update_near, 1) + second_pair[1] * residual / diagonal
        solution = solution + update
    return (solution, residual, update)


def relax(context, right_side, start, degree, lower, final):
    diagonal = inner(context[2], 1)
    centre, weights = chebyshev_coefs(degree, lower)
    if start is None:
        residual = right_side
    else:
        residual = right_side - operate_near(context, start)
    update = residual / (centre * diagonal)
    solution = update if start is None else start + update
    plan_list = list(weights) + ([None] if final else [])
    position = 0
    while position + 1 < len(plan_list):
        solution, residual, update = two_steps(
            context, solution, residual, update, plan_list[position], plan_list[position + 1]
        )
        position = position + 2
    leftover = plan_list[position:]
    for pair in leftover:
        residual = residual - operate_near(context, update)
        update = pair[0] * update + pair[1] * residual / diagonal
        solution = solution + update
    return (solution, residual)


def body(conductivity, source):
    coeff_now = conductivity
    contexts = []
    for grid_level in range(LEVELS):
        if grid_level > 0:
            coeff_now = coarsen(coeff_now)
        spacing = float(4**grid_level)
        coeff_ext = padded_2(coeff_now, (("gx", 0), ("gy", 1), ("gz", 2)), 2)
        inside = inside_mask(coeff_now.shape, 1)
        diagonal_ext = jnp.where(inside, diagonal_of(coeff_ext, spacing), 1.0)
        contexts.append((spacing, coeff_ext, diagonal_ext, inside))

    def cycle(grid_level, right_side):
        context = contexts[grid_level]
        if grid_level == LEVELS - 1:
            return relax(context, right_side, None, COARSE_DEGREE, coarse_low, False)
        solution, residual = relax(context, right_side, None, DEGREE, smooth_low, True)
        correction, ignored = cycle(grid_level + 1, coarsen(residual))
        solution = solution + refine(correction)
        return relax(context, right_side, solution, DEGREE, smooth_low, grid_level == 0)

    return cycle(0, source)


def cells(shape, dim):
    return lax.broadcasted_iota(jnp.int32, shape, dim)


def ones_where(condition):
    return jnp.where(condition, 1.0, 0.0).astype(jnp.bfloat16)


def pick(dense, chosen):
    total = None
    for _ in range(3):
        part = dense.astype(jnp.bfloat16)
        dense = dense - part.astype(jnp.float32)
        term = jnp.dot(part, chosen, preferred_element_type=jnp.float32)
        total = term if total is None else total + term
    return total


def turn(values, shift):
    dim = len(values.shape) - 1
    return pltpu.roll(values, shift % values.shape[dim], dim)


def beside(values):
    low, high = turn(values, 1), turn(values, -1)
    tiles = values.shape[0]
    if tiles > 1:
        lane = cells(values.shape, 2)
        low = jnp.where(lane == 0, jnp.concatenate([low[tiles - 1 :], low[: tiles - 1]]), low)
        high = jnp.where(lane == 127, jnp.concatenate([high[1:], high[:1]]), high)
    return low + high


FACE = 14.0 / 3.0


def around_of(before, here, after, tiles):
    faces = before[0] + after[0] + here[1]
    edges = before[1] + after[1]
    inward = FACE * here[0] + faces + (1.0 / 3.0) * edges
    return (FACE * faces + edges)[:tiles] + beside(inward)[:tiles]


class Level:
    def __init__(self, refs, scale):
        self.ks, self.r, self.dg, self.di = refs[:4]
        self.now, self.new = refs[4:6], refs[6:8]
        self.scale = scale

    def grab(self, ref, p, row):
        return (
            ref[p, :, row : row + 8, :],
            ref[p, :, row - 1 : row + 7, :] + ref[p, :, row + 1 : row + 9, :],
        )

    def diagonal(self, raw, span, rows):
        base, count = span
        for row in rows:
            at = slice(row, row + 8)
            before, here = self.grab(raw, base - 1, row), self.grab(raw, base, row)
            for p in (base + j for j in range(count)):
                after = self.grab(raw, p + 1, row)
                near = around_of(before, here, after, raw.shape[1])
                total = self.scale * (128.0 * here[0] + 3.0 * near)
                self.dg[p, :, at, :] = total
                self.di[p, :, at, :] = jnp.where(here[0] > 0.0, 1.0 / total, 0.0)
                self.ks[p, :, at, :] = (3.0 * self.scale) * here[0]
                before, here = here, after

    def first_update(self, span, rows, centre):
        base, count = span
        for row in rows:
            at = slice(row, row + 8)
            for p in (base + j for j in range(count)):
                fresh = self.r[p, :, at, :] * self.di[p, :, at, :] * (1.0 / centre)
                self.now[0][p, :, at, :] = fresh
                self.now[1][p, :, at, :] = fresh * self.ks[p, :, at, :]

    def apply(self, span, rows, pair, tiles=None):
        base, count = span
        tiles = tiles or self.r.shape[1]
        some = slice(0, tiles)
        for row in rows:
            at = slice(row, row + 8)
            before = [self.grab(ref, base - 1, row) for ref in self.now]
            here = [self.grab(ref, base, row) for ref in self.now]
            for p in (base + j for j in range(count)):
                after = [self.grab(ref, p + 1, row) for ref in self.now]
                plain, heavy = (around_of(*parts, tiles) for parts in zip(before, here, after))
                coeff = self.ks[p, some, at, :]
                field = here[0][0][:tiles]
                left = self.dg[p, some, at, :] * field - (coeff * plain + heavy)
                left = self.r[p, some, at, :] - left
                self.r[p, some, at, :] = left
                if pair is not None:
                    fresh = pair[1] * (left * self.di[p, some, at, :])
                    if pair[0] != 0.0:
                        fresh = pair[0] * field + fresh
                    self.new[0][p, some, at, :] = fresh
                    self.new[1][p, some, at, :] = coeff * fresh
                before, here = here, after
        self.now, self.new = self.new, self.now


def kernel(sizes, block, *refs):
    (nx, ny, nz) = sizes
    (bx, by, bz) = block
    deep = 5
    cx, cy = bx // 2, by // 2
    (k_in, b_in, x_out, r_out) = refs[:4]
    (k_raw, k_mid, k_low) = refs[4:7]
    fine = Level(refs[7:15], 0.5 / 30.0)
    mid = Level(refs[15:23], 0.5 / 4.0 / 30.0)
    low = Level(refs[23:31], 0.5 / 16.0 / 30.0)
    (r_near, x_fine, x_mid, x_low, half_sum) = refs[31:36]
    (k_send, b_send, k_edge, b_edge, k_side, b_side) = refs[36:42]
    (z_send, z_got, zr_send, zr_got) = refs[42:46]
    (load_sem, send_sem, k_sem, b_sem, r_sem, z_sem, zr_sem) = refs[46:53]
    (far_send, far_k, far_b) = refs[53:56]
    ix, iy, iz = lax.axis_index("gx"), lax.axis_index("gy"), lax.axis_index("gz")
    own = 1 + deep * ix
    other = (1 - ix, iy, iz)
    mine = (pl.ds(own, bx), pl.ds(0, 2), pl.ds(by, by), slice(None))

    def span(width):
        return (own - ix * width, bx + width)

    both, middle = (by // 2, by + by // 2), (by,)

    for ref, target, which in ((k_in, k_raw, 0), (b_in, fine.r, 1)):
        for t in range(2):
            pltpu.make_async_copy(
                ref.at[:, :, pl.ds(128 * t, 128)],
                target.at[pl.ds(own, bx), t, pl.ds(by, by), :],
                load_sem.at[which],
            ).start()

    barrier = pltpu.get_barrier_semaphore()
    z_there = {1: iz + 1 < nz, -1: iz > 0}
    y_there = {1: iy + 1 < ny, -1: iy > 0, 0: None}

    def when(*conditions):
        kept = [c for c in conditions if c is not None]
        if not kept:
            return lambda f: f()
        total = kept[0]
        for c in kept[1:]:
            total = total & c
        return pl.when(total)

    def column(skip):
        for jx in range(nx):
            for jy in range(ny):
                if jx or jy or not skip:
                    yield ((ix + jx) % nx, (iy + jy) % ny)

    def greet(target):
        pl.semaphore_signal(barrier, inc=1, device_id=target, device_id_type=MESH)

    for jx, jy in column(True):
        greet((jx, jy, iz))
    for dz in (1, -1):
        @when(z_there[dz])
        def _():
            for jx, jy in column(False):
                greet((jx, jy, iz + dz))

    def clear(ref, *at):
        for p in range(ref.shape[0]):
            ref[(p, *at)] = jnp.zeros(ref[(p, *at)].shape, jnp.float32)

    for p in (0, bx + deep + 1):
        k_raw[p] = jnp.zeros(k_raw.shape[1:], jnp.float32)
    for ref in (k_raw, fine.r, r_near):
        @pl.when(iy == 0)
        def _():
            clear(ref, slice(0, 2), slice(0, by))

        @pl.when(iy == ny - 1)
        def _():
            clear(ref, slice(0, 2), slice(2 * by, 3 * by))

    def blank(ref, dims):
        ref[dims] = jnp.zeros(ref[dims].shape, jnp.float32)

    for ref in (z_got, zr_got):
        for side, gone in ((0, iz == 0), (1, iz == nz - 1)):
            @pl.when(gone)
            def _():
                blank(ref, (side,))

        for j, gone in ((2, iy == 0), (0, iy == ny - 1)):
            @pl.when(gone)
            def _():
                for side in (0, 1):
                    blank(ref, (side, j))
    for ref in (k_side, b_side):
        for side, gone in ((0, iz == 0), (1, iz == nz - 1)):
            @pl.when(gone)
            def _():
                blank(ref, (side,))
    for ref in (*fine.now, *fine.new, *mid.now, *mid.new, *low.now, *low.new, k_low, x_mid):
        clear(ref)
    top = nx * cx + 1
    for p in (0, top):
        k_mid[p] = jnp.zeros(k_mid.shape[1:], jnp.float32)
    for row in (0, ny * cy + 1):
        clear(k_mid, slice(None), slice(row, row + 1))
    half_sum[...] = jnp.zeros(half_sum.shape, jnp.float32)

    lane = cells((8, 128), 1)
    shrink = ones_where(cells((256, 128), 0) >> 1 == cells((256, 128), 1))

    def wide(values):
        return jnp.concatenate([values[0], values[1]], axis=1)

    def coarse_block(ref, send, edge):
        for q in range(cx):
            p = own + 2 * q
            half_sum[q, :, 0:by, :] = (
                ref[p, 0:2, by : 2 * by, :] + ref[p + 1, 0:2, by : 2 * by, :]
            )
        rows = [
            wide(
                half_sum[q, :, pl.ds(0, by, stride=2), :]
                + half_sum[q, :, pl.ds(1, by, stride=2), :]
            )
            for q in range(cx)
        ]
        parts = (pick(jnp.concatenate(rows, axis=0), shrink) * 0.125).reshape(cx, by, 128)
        send[...] = parts
        low_part = parts[0]
        top_part = turn(parts[0], 32)
        for q in range(1, cx):
            here = (lane >> 5) == q
            low_part = jnp.where(here, turn(parts[q], 32 * q), low_part)
            top_part = jnp.where(here, turn(parts[q], 32 * q - 96), top_part)
        edge[0] = top_part
        edge[1] = low_part

    def pack_z(ref, kind, into):
        slot = lane >> 4
        front = (lane & 15) < 8
        packs = [jnp.zeros((8, 128), jnp.float32)] * 2 if into is None else into
        top, bottom = packs
        for q in range(bx):
            here = slot == q
            low_tile = ref[own + q, 0, by : 2 * by, :]
            top_tile = ref[own + q, 1, by : 2 * by, :]
            if kind == 0:
                top = jnp.where(here & front, turn(top_tile, 16 * q - 120), top)
                bottom = jnp.where(
                    here & jnp.logical_not(front), turn(low_tile, 16 * q + 8), bottom
                )
            else:
                after = slot == (q + 1) % 8
                top = jnp.where(
                    here & jnp.logical_not(front), turn(top_tile, 16 * q + 8 - 120), top
                )
                bottom = jnp.where(after & front, turn(low_tile, 16 * q + 16), bottom)
        return (top, bottom)

    def save_z(packs, send):
        for side in (0, 1):
            send[side, 0] = packs[side]
            moved = turn(packs[side], -16 * (bx - deep))
            send[side, 1] = jnp.where(ix == 0, moved, packs[side])

    def remote(source, target, out_sem, in_sem, device):
        return pltpu.make_async_remote_copy(
            src_ref=source,
            dst_ref=target,
            send_sem=out_sem,
            recv_sem=in_sem,
            device_id=device,
            device_id_type=MESH,
        )

    def near_views(ref, depth, dy, start_x, start_own, source):
        if dy == 0:
            rows = pl.ds(by, by)
        elif source:
            rows = pl.ds(2 * by - depth, depth) if dy == 1 else pl.ds(by, depth)
        else:
            rows = pl.ds(by - depth, depth) if dy == 1 else pl.ds(2 * by, depth)
        return [ref.at[pl.ds(start, planes), pl.ds(0, 2), rows, :]
                for start, planes in ((start_x, depth), (start_own, bx))]

    def near_start(source, target, depth, sems):
        start_from = jnp.where(ix == 0, bx + 1 - depth, deep + 1)
        start_to = jnp.where(ix == 0, deep + 1 - depth, bx + 1)
        for dy in (0, 1, -1):
            @when(y_there[dy])
            def _():
                froms = near_views(source, depth, dy, start_from, own, True)
                tos = near_views(target, depth, dy, start_to, own, False)
                args = (send_sem.at[0, dy + 1], sems.at[dy + 1])
                remote(froms[0], tos[0], *args, (1 - ix, iy + dy, iz)).start()
                if dy != 0:
                    remote(froms[1], tos[1], *args, (ix, iy + dy, iz)).start()

    def near_bytes(ref, depth, dy):
        if dy == 0:
            return ref.at[pl.ds(1, depth), pl.ds(0, 2), pl.ds(by, by), :]
        return ref.at[pl.ds(1, depth + bx), pl.ds(0, 2), pl.ds(by, depth), :]

    def near_wait(target, depth, sems):
        for dy in (0, 1, -1):
            @when(y_there[-dy])
            def _():
                view = near_bytes(target, depth, dy)
                remote(view, view, send_sem.at[0, dy + 1], sems.at[dy + 1], other).wait_recv()

    def near_sent(target, depths):
        for dy in (0, 1, -1):
            @when(y_there[dy])
            def _():
                for depth in depths:
                    view = near_bytes(target, depth, dy)
                    remote(view, view, send_sem.at[0, dy + 1], k_sem.at[dy + 1], other).wait_send()

    def z_start(send, got, sems):
        for side, dz in ((0, 1), (1, -1)):
            for dy in (0, 1, -1):
                @when(z_there[dz], y_there[dy])
                def _():
                    for xi in (0, 1):
                        remote(
                            send.at[side, xi],
                            got.at[side, dy + 1, xi],
                            send_sem.at[1 + side, dy + 1],
                            sems.at[side, dy + 1],
                            (ix if xi == 0 else 1 - ix, iy + dy, iz + dz),
                        ).start()

    def z_wait(got, sems, sent):
        for side, dz in ((0, 1), (1, -1)):
            for dy in (0, 1, -1):
                view = got.at[side, dy + 1]
                there = (z_there[dz], y_there[dy]) if sent else (z_there[-dz], y_there[-dy])

                @when(*there)
                def _():
                    args = (send_sem.at[1 + side, dy + 1], sems.at[side, dy + 1])
                    move = remote(view, view, *args, other)
                    if sent:
                        move.wait_send()
                    else:
                        move.wait_recv()

    def unpack_z(got, kind, target, count):
        front = (lane & 15) < 8
        kept = (lane < 8) | (lane >= 120)
        start_x = jnp.where(ix == 0, bx + 1, deep + 1 - count)
        skip = 0 if kind == 0 else 8
        for group in range(3):
            for xi, start, planes in ((0, own, bx), (1, None, deep)):
                lower, upper = got[0, 2 - group, xi], got[1, 2 - group, xi]
                pair = (lower, upper) if kind == 0 else (upper, lower)
                merged = jnp.where(front, *pair)
                first = own if xi == 0 else jnp.where(ix == 0, bx + 1, 1)
                for q in range(planes):
                    target[first + q, 2, by * group : by * group + by, :] = jnp.where(
                        kept, turn(merged, -(16 * q + 8 + skip)), 0.0
                    )

    def far_start(send, edge, target, side_target, sems):
        for jx, jy in column(True):
            remote(
                send.at[:, pl.ds(0, cy), :],
                target.at[pl.ds(1 + cx * ix, cx), 0, pl.ds(1 + cy * iy, cy), :],
                far_send.at[0],
                sems.at[0],
                (jx, jy, iz),
            ).start()
        for side, dz in ((0, 1), (1, -1)):
            @when(z_there[dz])
            def _():
                for jx, jy in column(False):
                    remote(
                        edge.at[side, pl.ds(0, cy), :],
                        side_target.at[side, ix, pl.ds(cy * iy, cy), :],
                        far_send.at[1 + side],
                        sems.at[1 + side],
                        (jx, jy, iz + dz),
                    ).start()

    def far_moves(target, side_target, sems, sent):
        view = target.at[pl.ds(1, nx * ny - 1), 0, pl.ds(1, cx * cy), :]
        move = remote(view, view, far_send.at[0], sems.at[0], other)
        yield None, move
        for side, dz in ((0, 1), (1, -1)):
            view = side_target.at[side]
            move = remote(view, view, far_send.at[1 + side], sems.at[1 + side], other)
            yield z_there[dz if sent else -dz], move

    def far_wait(target, side_target, sems):
        for there, move in far_moves(target, side_target, sems, False):
            when(there)(move.wait_recv)

    def far_sent(target, side_target, sems):
        for there, move in far_moves(target, side_target, sems, True):
            when(there)(move.wait_send)

    def keep_own(send, target):
        for jy in range(ny):
            @pl.when(iy == jy)
            def _():
                for q in range(cx):
                    rows = slice(1 + cy * jy, 1 + cy * jy + cy)
                    target[1 + cx * ix + q, 0, rows, :] = send[q, 0:cy, :]

    def unpack_far(side_target, target):
        shape = side_target.shape[2:]
        column_of = cells(shape, 1)
        for jx in range(nx):
            below, above = side_target[0, jx], side_target[1, jx]
            for q in range(cx):
                upper = jnp.where(column_of < 32, turn(above, -32 * q), 0.0)
                target[1 + cx * jx + q, 1, 1 : 1 + shape[0], :] = jnp.where(
                    column_of >= 96, turn(below, 96 - 32 * q), upper
                )

    for which, ref in ((0, k_raw), (1, fine.r)):
        view = ref.at[mine]
        pltpu.make_async_copy(view, view, load_sem.at[which]).wait()
    save_z(pack_z(fine.r, 1, pack_z(k_raw, 0, None)), z_send)
    coarse_block(k_raw, k_send, k_edge)

    peers = nx * ny - 1
    for dz in (1, -1):
        peers = peers + jnp.where(z_there[dz], nx * ny, 0)
    pl.semaphore_wait(barrier, peers)

    near_start(k_raw, k_raw, deep, k_sem)
    z_start(z_send, z_got, z_sem)
    near_start(fine.r, fine.r, deep - 1, b_sem)
    far_start(k_send, k_edge, k_mid, k_side, far_k)
    keep_own(k_send, k_mid)

    near_wait(k_raw, deep, k_sem)
    z_wait(z_got, z_sem, False)
    unpack_z(z_got, 0, k_raw, deep)
    fine.diagonal(k_raw, span(4), both)
    unpack_z(z_got, 1, fine.r, deep)
    near_wait(fine.r, deep - 1, b_sem)
    near_sent(fine.r, (deep, deep - 1))
    z_wait(z_got, z_sem, True)

    own_fine = [(q, own + q) for q in range(bx)]
    own_rows = slice(by, 2 * by)

    def add_fine(ref, fresh=False):
        for q, p in own_fine:
            value = ref[p, 0:2, own_rows, :]
            x_fine[q] = value if fresh else x_fine[q] + value

    def smooth_fine():
        for number in range(DEGREE):
            pair = weights[number] if number < DEGREE - 1 else None
            width = DEGREE - 1 - number
            fine.apply(span(width), both if width else middle, pair, None if width else 2)
            if pair is not None:
                add_fine(fine.now[0])

    centre, weights = chebyshev_coefs(DEGREE, smooth_low)
    fine.first_update(span(4), both, centre)
    add_fine(fine.now[0], True)
    smooth_fine()

    coarse_block(fine.r, b_send, b_edge)
    far_sent(k_mid, k_side, far_k)
    far_start(b_send, b_edge, mid.r, b_side, far_b)
    keep_own(b_send, mid.r)
    save_z(pack_z(fine.r, 0, None), zr_send)
    near_start(fine.r, r_near, deep - 1, r_sem)
    z_start(zr_send, zr_got, zr_sem)
    for q, p in own_fine:
        r_near[p, 0:2, own_rows, :] = fine.r[p, 0:2, own_rows, :]

    mid_span, mid_rows = (1, nx * cx), tuple(range(1, ny * cy, 8))
    low_span, low_rows = (1, nx * cx // 2), tuple(range(1, ny * cy // 2, 8))
    lows = nx * cx // 2
    low_row = ny * cy // 2

    def to_low(ref, target):
        rows = []
        for q in range(lows):
            total = None
            for p in (1 + 2 * q, 2 + 2 * q):
                for row in (1, 2):
                    part = ref[p, :, pl.ds(row, low_row, stride=2), :]
                    total = part if total is None else total + part
            rows.append(wide(total))
        parts = pick(jnp.concatenate(rows, axis=0), shrink) * 0.125
        target[1 : 1 + lows, 0, 1 : 1 + low_row, :] = parts.reshape(lows, low_row, 128)

    far_wait(k_mid, k_side, far_k)
    unpack_far(k_side, k_mid)
    mid.diagonal(k_mid, mid_span, mid_rows)
    to_low(k_mid, k_low)
    low.diagonal(k_low, low_span, low_rows)

    far_wait(mid.r, b_side, far_b)
    unpack_far(b_side, mid.r)
    start = 8
    inside = (slice(1, 1 + nx * cx), slice(None), slice(1, 1 + ny * cy))

    def add_mid(ref, fresh=False):
        for q in range(nx * cx):
            value = ref[1 + q, :, 1 : 1 + ny * cy, :]
            at = (q, slice(None), slice(start, start + ny * cy))
            x_mid[at] = value if fresh else x_mid[at] + value

    mid.first_update(mid_span, mid_rows, centre)
    add_mid(mid.now[0], True)
    for number in range(DEGREE):
        pair = weights[number] if number < DEGREE - 1 else None
        mid.apply(mid_span, mid_rows, pair)
        if pair is not None:
            add_mid(mid.now[0])

    to_low(mid.r, low.r)
    low_centre, low_weights = chebyshev_coefs(COARSE_DEGREE, coarse_low)
    low.first_update(low_span, low_rows, low_centre)

    def low_now():
        return low.now[0][1 : 1 + lows, 0, 1 : 1 + low_row, :]

    x_low[...] = low_now()
    for pair in low_weights:
        low.apply(low_span, low_rows, pair)
        x_low[...] += low_now()

    spread = ones_where(cells((128, 256), 0) == cells((128, 256), 1) >> 1)
    fixed = pick(x_low[...].reshape(lows * low_row, 128), spread).reshape(lows, low_row, 256)
    for q in range(lows):
        for t in range(2):
            value = fixed[q, :, 128 * t : 128 * t + 128]
            for p in (1 + 2 * q, 2 + 2 * q):
                for row in (1, 2):
                    mid.now[0][p, t, pl.ds(row, low_row, stride=2), :] = value
    for p in range(1, 1 + nx * cx):
        at = (p, slice(None), slice(1, 1 + ny * cy))
        mid.now[1][at] = mid.ks[at] * mid.now[0][at]
    add_mid(mid.now[0])
    mid.apply(mid_span, mid_rows, (0.0, 1.0 / centre))
    add_mid(mid.now[0])
    for pair in weights:
        mid.apply(mid_span, mid_rows, pair)
        add_mid(mid.now[0])

    near_wait(r_near, deep - 1, r_sem)
    z_wait(zr_got, zr_sem, False)
    unpack_z(zr_got, 0, r_near, deep)
    shape = (256, 384)
    from_lane, to_lane = cells(shape, 0), cells(shape, 1)
    to_lane = jnp.where(
        to_lane < 256, to_lane >> 1, (to_lane >> 1) + jnp.where(to_lane < 320, 0, 64)
    )
    widen = ones_where(from_lane == to_lane)
    planes = (bx + deep + 1) // 2
    rows = []
    x_rows = 16
    for j in range(planes):
        from_row = start - 3 + cy * iy
        rows.append(wide(x_mid[ix + j, :, pl.ds(from_row, x_rows), :]))
    fixed = pick(jnp.concatenate(rows, axis=0), widen).reshape(planes, x_rows, 384)
    for j in range(planes):
        for t in range(3):
            value = fixed[j, :, 128 * t : 128 * t + 128]
            for p in (0, 1):
                for row in (0, 1):
                    at = 1 - ix + 2 * j + p
                    fine.now[0][at, t, pl.ds(2 + row, 8, stride=2), :] = value[0:8]
                    fine.now[0][at, t, pl.ds(18 + row, 2, stride=2), :] = value[8:10]
    for p in range(1, 1 + bx + deep):
        fine.now[1][p] = (3.0 * fine.scale) * k_raw[p] * fine.now[0][p]
    add_fine(fine.now[0])
    fine.r = r_near
    fine.apply(span(4), both, (0.0, 1.0 / centre))
    add_fine(fine.now[0])
    smooth_fine()
    for q, p in own_fine:
        for t in range(2):
            x_out[q, :, 128 * t : 128 * t + 128] = x_fine[q, t]
            r_out[q, :, 128 * t : 128 * t + 128] = fine.r[p, t, own_rows, :]
    near_sent(r_near, (deep - 1,))
    z_wait(zr_got, zr_sem, True)
    far_sent(mid.r, b_side, far_b)


def gathered(sizes, conductivity, source):
    (nx, ny, nz) = sizes
    (bx, by, bz) = conductivity.shape
    kept = lambda *shape: pltpu.VMEM(shape, jnp.float32)
    fine = kept(bx + 7, 3, 3 * by, 128)
    mid = kept(nx * bx // 2 + 2, 2, ny * by // 2 + 8, 128)
    low = kept(nx * bx // 4 + 2, 1, ny * by // 4 + 8, 128)
    cx, cy = bx // 2, by // 2
    scratch = [fine, mid, low] + [fine] * 8 + [mid] * 8 + [low] * 8
    scratch += [fine, kept(bx, 2, by, 128), kept(nx * cx, 2, ny * cy + 24, 128)]
    scratch += [kept(nx * cx // 2, ny * cy // 2, 128), kept(cx, 2, 2 * by, 128)]
    scratch += [kept(cx, by, 128)] * 2 + [kept(2, by, 128)] * 2
    scratch += [kept(2, nx, ny * cy, 128)] * 2
    scratch += [kept(2, 2, by, 128), kept(2, 3, 2, by, 128)] * 2
    dma = pltpu.SemaphoreType.DMA
    scratch += [dma((2,)), dma((3, 3)), dma((3,)), dma((3,)), dma((3,)), dma((2, 3)), dma((2, 3))]
    scratch += [dma((3,)), dma((3,)), dma((3,))]
    shape = jax.ShapeDtypeStruct((bx, by, bz), jnp.float32)
    vmem = pl.BlockSpec(memory_space=pltpu.VMEM)
    anywhere = pl.BlockSpec(memory_space=pl.ANY)
    return pl.pallas_call(
        functools.partial(kernel, sizes, (bx, by, bz)),
        out_shape=(shape, shape),
        in_specs=[anywhere, anywhere],
        out_specs=(vmem, vmem),
        scratch_shapes=scratch,
        compiler_params=pltpu.CompilerParams(
            collective_id=0, has_side_effects=True, vmem_limit_bytes=48 * 1024 * 1024
        ),
    )(conductivity, source)


def plan(conductivity, source):
    sizes = tuple(lax.axis_size(axis) for axis in ("gx", "gy", "gz"))
    (bx, by, bz) = conductivity.shape
    fits = (bx, by, bz) == (8, 8, 256) and sizes[0] == 2 and sizes[1] == 4
    if fits:
        return gathered(sizes, conductivity, source)
    return body(conductivity, source)


def solution(mesh):
    in_specs = (P("gx", "gy", "gz"), P("gx", "gy", "gz"))
    out_specs = (P("gx", "gy", "gz"), P("gx", "gy", "gz"))
    return jax.shard_map(plan, mesh=mesh, in_specs=in_specs, out_specs=out_specs, check_vma=False)
```

time: 48.4 us -> 27.6 us (0.57)
  Pallas kernels: 44.2 us -> 23.8 us
    pallas_call x1, Pallas kernels: 44.2 us -> 23.8 us  [gathered(): pl.pallas_call(functools.partial(kernel, sizes, (bx, by, bz)), out_shape=...]
where the time goes in v1:
time: 27.6 us; the launch traced here: 27.4 us
  Pallas kernels  23.8 us (86%)
  local copies, waits for them, and re-layouts  2.93 us (11%)
  between operations  0.65 us (2%)
    pallas_call x1, Pallas kernels, gathered(): pl.pallas_call(functools.partial(kernel, sizes, (bx, by, bz)), out_shape=...  23.8 us
    unnamed x6, local copies, waits for them, and re-layouts  2.93 us

profile of v1, /device:TPU:1, one launch (start us, length us, event | category | flops | bytes accessed | tf_op | source)
XLA Modules:
  0.0 27.4 jit_solution(12628454400419601774)
XLA Ops:
  0.6 0.0 copy-start
  0.6 0.8 %copy-done = f32[8,8,256]{2,1,0:T(8,128)S(1)} copy-done((f32[8,8,256]{2,1,0:T(8,128)S(1)}, f32[8,8,256]{2,1,0:T(8,128)}, u32[]{:S(2)}) %copy-start) | copy-done | bytes 65560
  1.5 0.0 copy-start.1
  1.5 0.8 %copy-done.1 = f32[8,8,256]{2,1,0:T(8,128)S(1)} copy-done((f32[8,8,256]{2,1,0:T(8,128)S(1)}, f32[8,8,256]{2,1,0:T(8,128)}, u32[]{:S(2)}) %copy-start.1) | copy-done | bytes 65560
  2.3 23.8 %shard_map.41 = (f32[8,8,256]{2,1,0:T(8,128)S(1)}, f32[8,8,256]{2,1,0:T(8,128)S(1)}) custom-call(f32[8,8,256]{2,1,0:T(8,128)S(1)} %copy-done, f32[8,8,256]{2,1,0:T(8,128)S(1)} %copy-done.1), custom_call_target="tpu_custom_call" | custom-call | tf_op jit(solution)/shard_map/pallas_call | solution.py:813
  26.1 0.6 %copy.6 = f32[8,8,256]{2,1,0:T(8,128)} copy(f32[8,8,256]{2,1,0:T(8,128)S(1)} %get-tuple-element.4) | data formatting | bytes 131072
  26.8 0.6 %copy.7 = f32[8,8,256]{2,1,0:T(8,128)} copy(f32[8,8,256]{2,1,0:T(8,128)S(1)} %get-tuple-element.5) | data formatting | bytes 131072
Async XLA Ops:
  0.6 0.8 %copy-start = (f32[8,8,256]{2,1,0:T(8,128)S(1)}, f32[8,8,256]{2,1,0:T(8,128)}, u32[]{:S(2)}) copy-start(f32[8,8,256]{2,1,0:T(8,128)} %refs_0_.1) | copy-start | bytes 196612
  1.5 0.8 %copy-start.1 = (f32[8,8,256]{2,1,0:T(8,128)S(1)}, f32[8,8,256]{2,1,0:T(8,128)}, u32[]{:S(2)}) copy-start(f32[8,8,256]{2,1,0:T(8,128)} %refs_1_.1) | copy-start | bytes 196612

commit v2 on v1

--- a/solution.py
+++ b/solution.py
@@ -316,7 +316,7 @@
     (k_send, b_send, k_edge, b_edge, k_side, b_side) = refs[36:42]
     (z_send, z_got, zr_send, zr_got) = refs[42:46]
     (load_sem, send_sem, k_sem, b_sem, r_sem, z_sem, zr_sem) = refs[46:53]
-    (far_send, far_k, far_b) = refs[53:56]
+    (far_send, far_k, far_b, chain) = refs[53:57]
     ix, iy, iz = lax.axis_index("gx"), lax.axis_index("gy"), lax.axis_index("gz")
     own = 1 + deep * ix
     other = (1 - ix, iy, iz)
@@ -336,7 +336,7 @@
             ).start()
 
     barrier = pltpu.get_barrier_semaphore()
-    z_there = {1: iz + 1 < nz, -1: iz > 0}
+    z_there = {1: iz + 1 < nz, -1: iz > 0, 0: None}
     y_there = {1: iy + 1 < ny, -1: iy > 0, 0: None}
 
     def when(*conditions):
@@ -354,16 +354,27 @@
                 if jx or jy or not skip:
                     yield ((ix + jx) % nx, (iy + jy) % ny)
 
+    def counted(number, *conditions):
+        for c in conditions:
+            if c is not None:
+                number = jnp.where(c, number, 0)
+        return number
+
     def greet(target):
         pl.semaphore_signal(barrier, inc=1, device_id=target, device_id_type=MESH)
 
-    for jx, jy in column(True):
-        greet((jx, jy, iz))
-    for dz in (1, -1):
-        @when(z_there[dz])
-        def _():
-            for jx, jy in column(False):
-                greet((jx, jy, iz + dz))
+    peers = 0
+    for dz in (0, 1, -1):
+        for dy in (0, 1, -1):
+            there = (z_there[dz], y_there[dy])
+            near = [jx for jx in (ix, 1 - ix) if dz or dy or jx is not ix]
+
+            @when(*there)
+            def _():
+                for jx in near:
+                    greet((jx, iy + dy, iz + dz))
+
+            peers = peers + counted(len(near), *there)
 
     def clear(ref, *at):
         for p in range(ref.shape[0]):
@@ -435,8 +446,8 @@
             here = (lane >> 5) == q
             low_part = jnp.where(here, turn(parts[q], 32 * q), low_part)
             top_part = jnp.where(here, turn(parts[q], 32 * q - 96), top_part)
-        edge[0] = top_part
-        edge[1] = low_part
+        edge[0, 0:by] = top_part
+        edge[1, 0:by] = low_part
 
     def pack_z(ref, kind, into):
         slot = lane >> 4
@@ -625,18 +636,37 @@
         view = ref.at[mine]
         pltpu.make_async_copy(view, view, load_sem.at[which]).wait()
     save_z(pack_z(fine.r, 1, pack_z(k_raw, 0, None)), z_send)
+    pl.semaphore_wait(barrier, peers)
+
+    def pass_on(step):
+        for which, dy in ((0, 1), (1, -1)):
+            behind = iy - dy * step
+
+            @when(y_there[dy], behind >= 0, behind < ny)
+            def _():
+                pl.semaphore_signal(
+                    chain.at[which], inc=1, device_id=(ix, iy + dy, iz), device_id_type=MESH
+                )
+
+    def pass_wait(step):
+        for which, dy in ((0, 1), (1, -1)):
+            behind = iy - dy * (step + 1)
+
+            @when(behind >= 0, behind < ny)
+            def _():
+                pl.semaphore_wait(chain.at[which], 1)
+
+    pass_on(1)
+    z_start(z_send, z_got, z_sem)
+    near_start(k_raw, k_raw, deep, k_sem)
+    near_start(fine.r, fine.r, deep - 1, b_sem)
     coarse_block(k_raw, k_send, k_edge)
-
-    peers = nx * ny - 1
-    for dz in (1, -1):
-        peers = peers + jnp.where(z_there[dz], nx * ny, 0)
-    pl.semaphore_wait(barrier, peers)
-
-    near_start(k_raw, k_raw, deep, k_sem)
-    z_start(z_send, z_got, z_sem)
-    near_start(fine.r, fine.r, deep - 1, b_sem)
+    keep_own(k_send, k_mid)
+    for step in range(1, ny - 1):
+        pass_wait(step)
+        if step + 1 < ny - 1:
+            pass_on(step + 1)
     far_start(k_send, k_edge, k_mid, k_side, far_k)
-    keep_own(k_send, k_mid)
 
     near_wait(k_raw, deep, k_sem)
     z_wait(z_got, z_sem, False)
@@ -794,22 +824,22 @@
     (nx, ny, nz) = sizes
     (bx, by, bz) = conductivity.shape
     kept = lambda *shape: pltpu.VMEM(shape, jnp.float32)
-    fine = kept(bx + 7, 3, 3 * by, 128)
+    fine = kept(bx + 7, 3, 4 * by, 128)
     mid = kept(nx * bx // 2 + 2, 2, ny * by // 2 + 8, 128)
     low = kept(nx * bx // 4 + 2, 1, ny * by // 4 + 8, 128)
     cx, cy = bx // 2, by // 2
     scratch = [fine, mid, low] + [fine] * 8 + [mid] * 8 + [low] * 8
     scratch += [fine, kept(bx, 2, by, 128), kept(nx * cx, 2, ny * cy + 24, 128)]
     scratch += [kept(nx * cx // 2, ny * cy // 2, 128), kept(cx, 2, 2 * by, 128)]
-    scratch += [kept(cx, by, 128)] * 2 + [kept(2, by, 128)] * 2
+    scratch += [kept(cx, by, 128)] * 2 + [kept(2, 2 * by, 128)] * 2
     scratch += [kept(2, nx, ny * cy, 128)] * 2
     scratch += [kept(2, 2, by, 128), kept(2, 3, 2, by, 128)] * 2
     dma = pltpu.SemaphoreType.DMA
     scratch += [dma((2,)), dma((3, 3)), dma((3,)), dma((3,)), dma((3,)), dma((2, 3)), dma((2, 3))]
-    scratch += [dma((3,)), dma((3,)), dma((3,))]
-    shape = jax.ShapeDtypeStruct((bx, by, bz), jnp.float32)
+    scratch += [dma((3,)), dma((3,)), dma((3,)), pltpu.SemaphoreType.REGULAR((2,))]
+    shape = pltpu.VMEM((bx, by, bz), jnp.float32)
     vmem = pl.BlockSpec(memory_space=pltpu.VMEM)
-    anywhere = pl.BlockSpec(memory_space=pl.ANY)
+    anywhere = pl.BlockSpec(memory_space=pltpu.HBM)
     return pl.pallas_call(
         functools.partial(kernel, sizes, (bx, by, bz)),
         out_shape=(shape, shape),
@@ -817,7 +847,7 @@
         out_specs=(vmem, vmem),
         scratch_shapes=scratch,
         compiler_params=pltpu.CompilerParams(
-            collective_id=0, has_side_effects=True, vmem_limit_bytes=48 * 1024 * 1024
+            collective_id=0, has_side_effects=True, vmem_limit_bytes=66879488
         ),
     )(conductivity, source)
 

time: 27.6 us -> 26.2 us (0.949)
  local copies, waits for them, and re-layouts: 2.93 us -> 1.26 us
  Pallas kernels: 23.8 us -> 24.1 us
    unnamed x6 -> x2, local copies, waits for them, and re-layouts: 2.93 us -> 1.26 us
where the time goes in v2:
time: 26.2 us; the launch traced here: 26 us
  Pallas kernels  24.1 us (92%)
  local copies, waits for them, and re-layouts  1.26 us (5%)
  between operations  0.64 us (2%)
    pallas_call x1, Pallas kernels, gathered(): pl.pallas_call(functools.partial(kernel, sizes, (bx, by, bz)), out_shape=...  24.1 us
    unnamed x2, local copies, waits for them, and re-layouts  1.26 us

profile of v2, /device:TPU:1, one launch (start us, length us, event | category | flops | bytes accessed | tf_op | source)
XLA Modules:
  0.0 26.0 jit_solution(11418828971039165317)
XLA Ops:
  0.6 24.1 %shard_map.41 = (f32[8,8,256]{2,1,0:T(8,128)S(1)}, f32[8,8,256]{2,1,0:T(8,128)S(1)}) custom-call(f32[8,8,256]{2,1,0:T(8,128)} %refs_0_.1, f32[8,8,256]{2,1,0:T(8,128)} %refs_1_.1), custom_call_target="tpu_custom_call" | custom-call | tf_op jit(solution)/shard_map/pallas_call | solution.py:843
  24.7 0.6 %copy.6 = f32[8,8,256]{2,1,0:T(8,128)} copy(f32[8,8,256]{2,1,0:T(8,128)S(1)} %get-tuple-element.2) | data formatting | bytes 131072
  25.3 0.6 %copy.7 = f32[8,8,256]{2,1,0:T(8,128)} copy(f32[8,8,256]{2,1,0:T(8,128)S(1)} %get-tuple-element.3) | data formatting | bytes 131072

commit v3 on v2

--- a/solution.py
+++ b/solution.py
@@ -272,7 +272,9 @@
         for row in rows:
             at = slice(row, row + 8)
             for p in (base + j for j in range(count)):
-                fresh = self.r[p, :, at, :] * self.di[p, :, at, :] * (1.0 / centre)
+                scaled = self.r[p, :, at, :] * self.di[p, :, at, :]
+                self.r[p, :, at, :] = scaled
+                fresh = scaled * (1.0 / centre)
                 self.now[0][p, :, at, :] = fresh
                 self.now[1][p, :, at, :] = fresh * self.ks[p, :, at, :]
 
@@ -289,11 +291,11 @@
                 plain, heavy = (around_of(*parts, tiles) for parts in zip(before, here, after))
                 coeff = self.ks[p, some, at, :]
                 field = here[0][0][:tiles]
-                left = self.dg[p, some, at, :] * field - (coeff * plain + heavy)
+                left = field - self.di[p, some, at, :] * (coeff * plain + heavy)
                 left = self.r[p, some, at, :] - left
                 self.r[p, some, at, :] = left
                 if pair is not None:
-                    fresh = pair[1] * (left * self.di[p, some, at, :])
+                    fresh = pair[1] * left
                     if pair[0] != 0.0:
                         fresh = pair[0] * field + fresh
                     self.new[0][p, some, at, :] = fresh
@@ -315,8 +317,7 @@
     (r_near, x_fine, x_mid, x_low, half_sum) = refs[31:36]
     (k_send, b_send, k_edge, b_edge, k_side, b_side) = refs[36:42]
     (z_send, z_got, zr_send, zr_got) = refs[42:46]
-    (load_sem, send_sem, k_sem, b_sem, r_sem, z_sem, zr_sem) = refs[46:53]
-    (far_send, far_k, far_b, chain) = refs[53:57]
+    (load_sem, near_send, near_sem, z_sem, zr_sem, far_send, far_sem, chain) = refs[46:54]
     ix, iy, iz = lax.axis_index("gx"), lax.axis_index("gy"), lax.axis_index("gz")
     own = 1 + deep * ix
     other = (1 - ix, iy, iz)
@@ -327,7 +328,7 @@
 
     both, middle = (by // 2, by + by // 2), (by,)
 
-    for ref, target, which in ((k_in, k_raw, 0), (b_in, fine.r, 1)):
+    for ref, target, which in ((k_in, k_raw, 0), (b_in, r_near, 1), (b_in, fine.r, 2)):
         for t in range(2):
             pltpu.make_async_copy(
                 ref.at[:, :, pl.ds(128 * t, 128)],
@@ -419,18 +420,20 @@
         clear(k_mid, slice(None), slice(row, row + 1))
     half_sum[...] = jnp.zeros(half_sum.shape, jnp.float32)
 
+    own_rows = slice(by, 2 * by)
     lane = cells((8, 128), 1)
+
+    def residual_of(p):
+        return fine.r[p, 0:2, own_rows, :] * fine.dg[p, 0:2, own_rows, :]
     shrink = ones_where(cells((256, 128), 0) >> 1 == cells((256, 128), 1))
 
     def wide(values):
         return jnp.concatenate([values[0], values[1]], axis=1)
 
-    def coarse_block(ref, send, edge):
+    def coarse_block(read, send, edge):
         for q in range(cx):
             p = own + 2 * q
-            half_sum[q, :, 0:by, :] = (
-                ref[p, 0:2, by : 2 * by, :] + ref[p + 1, 0:2, by : 2 * by, :]
-            )
+            half_sum[q, :, 0:by, :] = read(p) + read(p + 1)
         rows = [
             wide(
                 half_sum[q, :, pl.ds(0, by, stride=2), :]
@@ -487,48 +490,73 @@
             device_id_type=MESH,
         )
 
-    def near_views(ref, depth, dy, start_x, start_own, source):
+    def near_views(ref, depth, dy, start_x, source):
         if dy == 0:
             rows = pl.ds(by, by)
         elif source:
             rows = pl.ds(2 * by - depth, depth) if dy == 1 else pl.ds(by, depth)
         else:
             rows = pl.ds(by - depth, depth) if dy == 1 else pl.ds(2 * by, depth)
-        return [ref.at[pl.ds(start, planes), pl.ds(0, 2), rows, :]
-                for start, planes in ((start_x, depth), (start_own, bx))]
-
-    def near_start(source, target, depth, sems):
+        return [
+            ref.at[pl.ds(start, planes), pl.ds(0, 2), rows, :]
+            for start, planes in ((start_x, depth), (own, bx))
+        ]
+
+    def near_start(source, target, depth, along_x, in_sem):
         start_from = jnp.where(ix == 0, bx + 1 - depth, deep + 1)
         start_to = jnp.where(ix == 0, deep + 1 - depth, bx + 1)
-        for dy in (0, 1, -1):
+        for dy in (0, 1, -1) if along_x else (1, -1):
             @when(y_there[dy])
             def _():
-                froms = near_views(source, depth, dy, start_from, own, True)
-                tos = near_views(target, depth, dy, start_to, own, False)
-                args = (send_sem.at[0, dy + 1], sems.at[dy + 1])
-                remote(froms[0], tos[0], *args, (1 - ix, iy + dy, iz)).start()
-                if dy != 0:
-                    remote(froms[1], tos[1], *args, (ix, iy + dy, iz)).start()
-
-    def near_bytes(ref, depth, dy):
-        if dy == 0:
-            return ref.at[pl.ds(1, depth), pl.ds(0, 2), pl.ds(by, by), :]
-        return ref.at[pl.ds(1, depth + bx), pl.ds(0, 2), pl.ds(by, depth), :]
-
-    def near_wait(target, depth, sems):
-        for dy in (0, 1, -1):
-            @when(y_there[-dy])
-            def _():
-                view = near_bytes(target, depth, dy)
-                remote(view, view, send_sem.at[0, dy + 1], sems.at[dy + 1], other).wait_recv()
-
-    def near_sent(target, depths):
-        for dy in (0, 1, -1):
-            @when(y_there[dy])
-            def _():
-                for depth in depths:
-                    view = near_bytes(target, depth, dy)
-                    remote(view, view, send_sem.at[0, dy + 1], k_sem.at[dy + 1], other).wait_send()
+                which = 0 if along_x else 1
+                remote(
+                    near_views(source, depth, dy, start_from, True)[which],
+                    near_views(target, depth, dy, start_to, False)[which],
+                    near_send.at[0],
+                    in_sem,
+                    (1 - ix if along_x else ix, iy + dy, iz),
+                ).start()
+
+    inner_y = (iy > 0) & (iy + 1 < ny)
+    inner_z = (iz > 0) & (iz + 1 < nz)
+
+    def part_of(ref, rows):
+        (p, t, n) = ref.shape[:3]
+        sizes = [
+            (a, b, rows // (a * b))
+            for a in range(1, p + 1)
+            for b in range(1, t + 1)
+            if rows % (a * b) == 0 and rows // (a * b) <= n
+        ]
+        (a, b, c) = sizes[0]
+        return ref.at[pl.ds(0, a), pl.ds(0, b), pl.ds(0, c), :]
+
+    def wait_rows(ref, out_sem, in_sem, sent, inner, base, each):
+        for condition, number in ((inner, 2), (jnp.logical_not(inner), 1)):
+            @pl.when(condition)
+            def _():
+                view = part_of(ref, base + number * each)
+                move = remote(view, view, out_sem, in_sem, other)
+                if sent:
+                    move.wait_send()
+                else:
+                    move.wait_recv()
+
+    def near_rows(depth, along_x):
+        if along_x:
+            return 2 * depth * by, 2 * depth * depth
+        return 0, 2 * bx * depth
+
+    def near_wait(depth, kinds, in_sem):
+        base = sum(near_rows(depth, kind)[0] for kind in kinds)
+        each = sum(near_rows(depth, kind)[1] for kind in kinds)
+        wait_rows(k_raw, near_send.at[0], in_sem, False, inner_y, base, each)
+
+    def near_sent(depths):
+        for depth in depths:
+            kinds = [near_rows(depth, kind) for kind in (True, False)]
+            base, each = sum(k[0] for k in kinds), sum(k[1] for k in kinds)
+            wait_rows(k_raw, near_send.at[0], near_sem.at[0], True, inner_y, base, each)
 
     def z_start(send, got, sems):
         for side, dz in ((0, 1), (1, -1)):
@@ -539,25 +567,17 @@
                         remote(
                             send.at[side, xi],
                             got.at[side, dy + 1, xi],
-                            send_sem.at[1 + side, dy + 1],
-                            sems.at[side, dy + 1],
+                            near_send.at[1 + side],
+                            sems.at[side],
                             (ix if xi == 0 else 1 - ix, iy + dy, iz + dz),
                         ).start()
 
-    def z_wait(got, sems, sent):
+    def z_wait(sems, sent):
         for side, dz in ((0, 1), (1, -1)):
-            for dy in (0, 1, -1):
-                view = got.at[side, dy + 1]
-                there = (z_there[dz], y_there[dy]) if sent else (z_there[-dz], y_there[-dy])
-
-                @when(*there)
-                def _():
-                    args = (send_sem.at[1 + side, dy + 1], sems.at[side, dy + 1])
-                    move = remote(view, view, *args, other)
-                    if sent:
-                        move.wait_send()
-                    else:
-                        move.wait_recv()
+            @pl.when(z_there[dz if sent else -dz])
+            def _():
+                args = (near_send.at[1 + side], sems.at[side], sent, inner_y, 2 * by, 2 * by)
+                wait_rows(k_raw, *args)
 
     def unpack_z(got, kind, target, count):
         front = (lane & 15) < 8
@@ -575,13 +595,13 @@
                         kept, turn(merged, -(16 * q + 8 + skip)), 0.0
                     )
 
-    def far_start(send, edge, target, side_target, sems):
+    def far_start(send, edge, target, side_target, in_sem):
         for jx, jy in column(True):
             remote(
                 send.at[:, pl.ds(0, cy), :],
                 target.at[pl.ds(1 + cx * ix, cx), 0, pl.ds(1 + cy * iy, cy), :],
                 far_send.at[0],
-                sems.at[0],
+                in_sem,
                 (jx, jy, iz),
             ).start()
         for side, dz in ((0, 1), (1, -1)):
@@ -591,27 +611,14 @@
                     remote(
                         edge.at[side, pl.ds(0, cy), :],
                         side_target.at[side, ix, pl.ds(cy * iy, cy), :],
-                        far_send.at[1 + side],
-                        sems.at[1 + side],
+                        far_send.at[0],
+                        in_sem,
                         (jx, jy, iz + dz),
                     ).start()
 
-    def far_moves(target, side_target, sems, sent):
-        view = target.at[pl.ds(1, nx * ny - 1), 0, pl.ds(1, cx * cy), :]
-        move = remote(view, view, far_send.at[0], sems.at[0], other)
-        yield None, move
-        for side, dz in ((0, 1), (1, -1)):
-            view = side_target.at[side]
-            move = remote(view, view, far_send.at[1 + side], sems.at[1 + side], other)
-            yield z_there[dz if sent else -dz], move
-
-    def far_wait(target, side_target, sems):
-        for there, move in far_moves(target, side_target, sems, False):
-            when(there)(move.wait_recv)
-
-    def far_sent(target, side_target, sems):
-        for there, move in far_moves(target, side_target, sems, True):
-            when(there)(move.wait_send)
+    def far_wait(in_sem, sent=False):
+        main, each = (nx * ny - 1) * cx * cy, nx * ny * cy
+        wait_rows(k_raw, far_send.at[0], in_sem, sent, inner_z, main, each)
 
     def keep_own(send, target):
         for jy in range(ny):
@@ -632,7 +639,7 @@
                     column_of >= 96, turn(below, 96 - 32 * q), upper
                 )
 
-    for which, ref in ((0, k_raw), (1, fine.r)):
+    for which, ref in ((0, k_raw), (1, r_near), (2, fine.r)):
         view = ref.at[mine]
         pltpu.make_async_copy(view, view, load_sem.at[which]).wait()
     save_z(pack_z(fine.r, 1, pack_z(k_raw, 0, None)), z_send)
@@ -658,53 +665,62 @@
 
     pass_on(1)
     z_start(z_send, z_got, z_sem)
-    near_start(k_raw, k_raw, deep, k_sem)
-    near_start(fine.r, fine.r, deep - 1, b_sem)
-    coarse_block(k_raw, k_send, k_edge)
+    near_start(k_raw, k_raw, deep, True, near_sem.at[0])
+    near_start(k_raw, k_raw, deep, False, near_sem.at[0])
+    near_start(r_near, fine.r, deep - 1, False, near_sem.at[1])
+    near_start(r_near, fine.r, deep - 1, True, near_sem.at[2])
+    coarse_block(lambda p: k_raw[p, 0:2, own_rows, :], k_send, k_edge)
     keep_own(k_send, k_mid)
     for step in range(1, ny - 1):
         pass_wait(step)
         if step + 1 < ny - 1:
             pass_on(step + 1)
-    far_start(k_send, k_edge, k_mid, k_side, far_k)
-
-    near_wait(k_raw, deep, k_sem)
-    z_wait(z_got, z_sem, False)
+    far_start(k_send, k_edge, k_mid, k_side, far_sem.at[0])
+
+    near_wait(deep, (True, False), near_sem.at[0])
+    z_wait(z_sem, False)
     unpack_z(z_got, 0, k_raw, deep)
     fine.diagonal(k_raw, span(4), both)
     unpack_z(z_got, 1, fine.r, deep)
-    near_wait(fine.r, deep - 1, b_sem)
-    near_sent(fine.r, (deep, deep - 1))
-    z_wait(z_got, z_sem, True)
-
-    own_fine = [(q, own + q) for q in range(bx)]
-    own_rows = slice(by, 2 * by)
-
-    def add_fine(ref, fresh=False):
-        for q, p in own_fine:
-            value = ref[p, 0:2, own_rows, :]
+    near_wait(deep - 1, (False,), near_sem.at[1])
+
+    def strip(first, last):
+        return (bx - last + ix * (deep + 1 + first - bx + last), last - first + 1)
+
+    def add_fine(ref, first=0, last=bx - 1, fresh=False):
+        for a in range(first, last + 1):
+            q = bx - 1 - a + ix * (2 * a - bx + 1)
+            value = ref[own + q, 0:2, own_rows, :]
             x_fine[q] = value if fresh else x_fine[q] + value
 
-    def smooth_fine():
+    def smooth_fine(first, last, grow):
         for number in range(DEGREE):
             pair = weights[number] if number < DEGREE - 1 else None
-            width = DEGREE - 1 - number
-            fine.apply(span(width), both if width else middle, pair, None if width else 2)
+            rows, tiles = (both, None) if number < DEGREE - 1 else (middle, 2)
+            fine.apply(strip(first, last), rows, pair, tiles)
             if pair is not None:
-                add_fine(fine.now[0])
+                add_fine(fine.now[0], max(first, 0), min(last, bx - 1))
+            first, last = first + 1, last + grow
 
     centre, weights = chebyshev_coefs(DEGREE, smooth_low)
-    fine.first_update(span(4), both, centre)
-    add_fine(fine.now[0], True)
-    smooth_fine()
-
-    coarse_block(fine.r, b_send, b_edge)
-    far_sent(k_mid, k_side, far_k)
-    far_start(b_send, b_edge, mid.r, b_side, far_b)
+    fine.first_update(strip(0, bx - 1), both, centre)
+    add_fine(fine.now[0], fresh=True)
+    smooth_fine(1, bx - 1, 0)
+    near_wait(deep - 1, (True,), near_sem.at[2])
+    fine.first_update(strip(-DEGREE, -1), both, centre)
+    smooth_fine(1 - DEGREE, 0, 1)
+
+    near_sent((deep, deep - 1))
+    z_wait(z_sem, True)
+    coarse_block(residual_of, b_send, b_edge)
+    far_wait(far_sem.at[0], True)
+    far_start(b_send, b_edge, mid.r, b_side, far_sem.at[1])
     keep_own(b_send, mid.r)
     save_z(pack_z(fine.r, 0, None), zr_send)
-    near_start(fine.r, r_near, deep - 1, r_sem)
     z_start(zr_send, zr_got, zr_sem)
+    near_start(fine.r, r_near, deep - 1, True, near_sem.at[3])
+    near_start(fine.r, r_near, deep - 1, False, near_sem.at[3])
+    own_fine = [(q, own + q) for q in range(bx)]
     for q, p in own_fine:
         r_near[p, 0:2, own_rows, :] = fine.r[p, 0:2, own_rows, :]
 
@@ -713,25 +729,25 @@
     lows = nx * cx // 2
     low_row = ny * cy // 2
 
-    def to_low(ref, target):
+    def to_low(read, target):
         rows = []
         for q in range(lows):
             total = None
             for p in (1 + 2 * q, 2 + 2 * q):
                 for row in (1, 2):
-                    part = ref[p, :, pl.ds(row, low_row, stride=2), :]
+                    part = read(p, pl.ds(row, low_row, stride=2))
                     total = part if total is None else total + part
             rows.append(wide(total))
         parts = pick(jnp.concatenate(rows, axis=0), shrink) * 0.125
         target[1 : 1 + lows, 0, 1 : 1 + low_row, :] = parts.reshape(lows, low_row, 128)
 
-    far_wait(k_mid, k_side, far_k)
+    far_wait(far_sem.at[0])
     unpack_far(k_side, k_mid)
     mid.diagonal(k_mid, mid_span, mid_rows)
-    to_low(k_mid, k_low)
+    to_low(lambda p, rows: k_mid[p, :, rows, :], k_low)
     low.diagonal(k_low, low_span, low_rows)
 
-    far_wait(mid.r, b_side, far_b)
+    far_wait(far_sem.at[1])
     unpack_far(b_side, mid.r)
     start = 8
     inside = (slice(1, 1 + nx * cx), slice(None), slice(1, 1 + ny * cy))
@@ -750,7 +766,7 @@
         if pair is not None:
             add_mid(mid.now[0])
 
-    to_low(mid.r, low.r)
+    to_low(lambda p, rows: mid.r[p, :, rows, :] * mid.dg[p, :, rows, :], low.r)
     low_centre, low_weights = chebyshev_coefs(COARSE_DEGREE, coarse_low)
     low.first_update(low_span, low_rows, low_centre)
 
@@ -780,8 +796,8 @@
         mid.apply(mid_span, mid_rows, pair)
         add_mid(mid.now[0])
 
-    near_wait(r_near, deep - 1, r_sem)
-    z_wait(zr_got, zr_sem, False)
+    near_wait(deep - 1, (True, False), near_sem.at[3])
+    z_wait(zr_sem, False)
     unpack_z(zr_got, 0, r_near, deep)
     shape = (256, 384)
     from_lane, to_lane = cells(shape, 0), cells(shape, 1)
@@ -810,14 +826,14 @@
     fine.r = r_near
     fine.apply(span(4), both, (0.0, 1.0 / centre))
     add_fine(fine.now[0])
-    smooth_fine()
+    smooth_fine(1 - DEGREE, bx - 1, 0)
     for q, p in own_fine:
         for t in range(2):
             x_out[q, :, 128 * t : 128 * t + 128] = x_fine[q, t]
-            r_out[q, :, 128 * t : 128 * t + 128] = fine.r[p, t, own_rows, :]
-    near_sent(r_near, (deep - 1,))
-    z_wait(zr_got, zr_sem, True)
-    far_sent(mid.r, b_side, far_b)
+            r_out[q, :, 128 * t : 128 * t + 128] = residual_of(p)[t]
+    near_sent((deep - 1,))
+    z_wait(zr_sem, True)
+    far_wait(far_sem.at[1], True)
 
 
 def gathered(sizes, conductivity, source):
@@ -835,8 +851,8 @@
     scratch += [kept(2, nx, ny * cy, 128)] * 2
     scratch += [kept(2, 2, by, 128), kept(2, 3, 2, by, 128)] * 2
     dma = pltpu.SemaphoreType.DMA
-    scratch += [dma((2,)), dma((3, 3)), dma((3,)), dma((3,)), dma((3,)), dma((2, 3)), dma((2, 3))]
-    scratch += [dma((3,)), dma((3,)), dma((3,)), pltpu.SemaphoreType.REGULAR((2,))]
+    scratch += [dma((3,)), dma((3,)), dma((4,)), dma((2,)), dma((2,)), dma((1,)), dma((2,))]
+    scratch += [pltpu.SemaphoreType.REGULAR((2,))]
     shape = pltpu.VMEM((bx, by, bz), jnp.float32)
     vmem = pl.BlockSpec(memory_space=pltpu.VMEM)
     anywhere = pl.BlockSpec(memory_space=pltpu.HBM)

time: 26.2 us -> 25.3 us (0.966)
  Pallas kernels: 24.1 us -> 23.2 us
    pallas_call x1, Pallas kernels: 24.1 us -> 23.2 us  [gathered(): pl.pallas_call(functools.partial(kernel, sizes, (bx, by, bz)), out_shape=...]
where the time goes in v3:
time: 25.3 us; the launch traced here: 25.1 us
  Pallas kernels  23.2 us (92%)
  local copies, waits for them, and re-layouts  1.26 us (5%)
  between operations  0.64 us (3%)
    pallas_call x1, Pallas kernels, gathered(): pl.pallas_call(functools.partial(kernel, sizes, (bx, by, bz)), out_shape=...  23.2 us
    unnamed x2, local copies, waits for them, and re-layouts  1.26 us

profile of v3, /device:TPU:1, one launch (start us, length us, event | category | flops | bytes accessed | tf_op | source)
XLA Modules:
  0.0 25.1 jit_solution(13815229975087278127)
XLA Ops:
  0.6 23.2 %shard_map.41 = (f32[8,8,256]{2,1,0:T(8,128)S(1)}, f32[8,8,256]{2,1,0:T(8,128)S(1)}) custom-call(f32[8,8,256]{2,1,0:T(8,128)} %refs_0_.1, f32[8,8,256]{2,1,0:T(8,128)} %refs_1_.1), custom_call_target="tpu_custom_call" | custom-call | tf_op jit(solution)/shard_map/pallas_call | solution.py:859
  23.9 0.6 %copy.6 = f32[8,8,256]{2,1,0:T(8,128)} copy(f32[8,8,256]{2,1,0:T(8,128)S(1)} %get-tuple-element.2) | data formatting | bytes 131072
  24.5 0.6 %copy.7 = f32[8,8,256]{2,1,0:T(8,128)} copy(f32[8,8,256]{2,1,0:T(8,128)S(1)} %get-tuple-element.3) | data formatting | bytes 131072

commit v4 on v3

--- a/solution.py
+++ b/solution.py
@@ -309,15 +309,16 @@
     (bx, by, bz) = block
     deep = 5
     cx, cy = bx // 2, by // 2
-    (k_in, b_in, x_out, r_out) = refs[:4]
+    (k_in, b_in, x_out, r_out, d_out) = refs[:5]
+    refs = refs[1:]
     (k_raw, k_mid, k_low) = refs[4:7]
     fine = Level(refs[7:15], 0.5 / 30.0)
     mid = Level(refs[15:23], 0.5 / 4.0 / 30.0)
     low = Level(refs[23:31], 0.5 / 16.0 / 30.0)
     (r_near, x_fine, x_mid, x_low, half_sum) = refs[31:36]
     (k_send, b_send, k_edge, b_edge, k_side, b_side) = refs[36:42]
-    (z_send, z_got, zr_send, zr_got) = refs[42:46]
-    (load_sem, near_send, near_sem, z_sem, zr_sem, far_send, far_sem, chain) = refs[46:54]
+    (z_send, z_passed, z_got, zr_send, zr_passed, zr_got) = refs[42:48]
+    (load_sem, near_send, near_sem, z_sem, zr_sem, far_send, far_sem, chain) = refs[48:56]
     ix, iy, iz = lax.axis_index("gx"), lax.axis_index("gy"), lax.axis_index("gz")
     own = 1 + deep * ix
     other = (1 - ix, iy, iz)
@@ -365,10 +366,10 @@
         pl.semaphore_signal(barrier, inc=1, device_id=target, device_id_type=MESH)
 
     peers = 0
-    for dz in (0, 1, -1):
-        for dy in (0, 1, -1):
+    for dz, dys in ((0, (0, 1, -1)), (1, (0,)), (-1, (0,))):
+        for dy in dys:
             there = (z_there[dz], y_there[dy])
-            near = [jx for jx in (ix, 1 - ix) if dz or dy or jx is not ix]
+            near = [ix] if dz else [jx for jx in (ix, 1 - ix) if dy or jx is not ix]
 
             @when(*there)
             def _():
@@ -395,11 +396,12 @@
     def blank(ref, dims):
         ref[dims] = jnp.zeros(ref[dims].shape, jnp.float32)
 
-    for ref in (z_got, zr_got):
+    for ref, passed in ((z_got, z_passed), (zr_got, zr_passed)):
         for side, gone in ((0, iz == 0), (1, iz == nz - 1)):
             @pl.when(gone)
             def _():
                 blank(ref, (side,))
+                blank(passed, (side,))
 
         for j, gone in ((2, iy == 0), (0, iy == ny - 1)):
             @pl.when(gone)
@@ -430,7 +432,7 @@
     def wide(values):
         return jnp.concatenate([values[0], values[1]], axis=1)
 
-    def coarse_block(read, send, edge):
+    def coarse_block(read, send):
         for q in range(cx):
             p = own + 2 * q
             half_sum[q, :, 0:by, :] = read(p) + read(p + 1)
@@ -443,6 +445,9 @@
         ]
         parts = (pick(jnp.concatenate(rows, axis=0), shrink) * 0.125).reshape(cx, by, 128)
         send[...] = parts
+        return parts
+
+    def coarse_edge(parts, edge):
         low_part = parts[0]
         top_part = turn(parts[0], 32)
         for q in range(1, cx):
@@ -558,35 +563,59 @@
             base, each = sum(k[0] for k in kinds), sum(k[1] for k in kinds)
             wait_rows(k_raw, near_send.at[0], near_sem.at[0], True, inner_y, base, each)
 
-    def z_start(send, got, sems):
+    def z_start(send, passed, sems):
         for side, dz in ((0, 1), (1, -1)):
-            for dy in (0, 1, -1):
-                @when(z_there[dz], y_there[dy])
+            @pl.when(z_there[dz])
+            def _():
+                remote(
+                    send.at[side],
+                    passed.at[side],
+                    near_send.at[1 + side],
+                    sems.at[side],
+                    (ix, iy, iz + dz),
+                ).start()
+
+    def z_pass_on(passed, got, sems):
+        for side, dz in ((0, 1), (1, -1)):
+            @pl.when(z_there[-dz])
+            def _():
+                view = passed.at[side]
+                remote(view, view, near_send.at[1 + side], sems.at[side], other).wait_recv()
+                for dy in (0, 1, -1):
+                    @when(y_there[dy])
+                    def _():
+                        for xi in (0, 1) if dy else (1,):
+                            remote(
+                                passed.at[side, xi],
+                                got.at[side, dy + 1, xi],
+                                near_send.at[3 + side],
+                                sems.at[2 + side],
+                                (ix if xi == 0 else 1 - ix, iy + dy, iz),
+                            ).start()
+
+    def z_wait(passed, sems, sent):
+        for side, dz in ((0, 1), (1, -1)):
+            @pl.when(z_there[-dz])
+            def _():
+                args = (near_send.at[3 + side], sems.at[2 + side], sent, inner_y, by, 2 * by)
+                wait_rows(k_raw, *args)
+
+            if sent:
+                @pl.when(z_there[dz])
                 def _():
-                    for xi in (0, 1):
-                        remote(
-                            send.at[side, xi],
-                            got.at[side, dy + 1, xi],
-                            near_send.at[1 + side],
-                            sems.at[side],
-                            (ix if xi == 0 else 1 - ix, iy + dy, iz + dz),
-                        ).start()
-
-    def z_wait(sems, sent):
-        for side, dz in ((0, 1), (1, -1)):
-            @pl.when(z_there[dz if sent else -dz])
-            def _():
-                args = (near_send.at[1 + side], sems.at[side], sent, inner_y, 2 * by, 2 * by)
-                wait_rows(k_raw, *args)
-
-    def unpack_z(got, kind, target, count):
+                    view = passed.at[side]
+                    remote(view, view, near_send.at[1 + side], sems.at[side], other).wait_send()
+
+    def unpack_z(passed, got, kind, target):
         front = (lane & 15) < 8
         kept = (lane < 8) | (lane >= 120)
-        start_x = jnp.where(ix == 0, bx + 1, deep + 1 - count)
         skip = 0 if kind == 0 else 8
         for group in range(3):
-            for xi, start, planes in ((0, own, bx), (1, None, deep)):
-                lower, upper = got[0, 2 - group, xi], got[1, 2 - group, xi]
+            for xi, planes in ((0, bx), (1, deep)):
+                straight = group == 1 and xi == 0
+                lower, upper = (
+                    passed[side, 0] if straight else got[side, 2 - group, xi] for side in (0, 1)
+                )
                 pair = (lower, upper) if kind == 0 else (upper, lower)
                 merged = jnp.where(front, *pair)
                 first = own if xi == 0 else jnp.where(ix == 0, bx + 1, 1)
@@ -595,8 +624,8 @@
                         kept, turn(merged, -(16 * q + 8 + skip)), 0.0
                     )
 
-    def far_start(send, edge, target, side_target, in_sem):
-        for jx, jy in column(True):
+    def far_start(send, target, in_sem):
+        for jx, jy in reversed(list(column(True))):
             remote(
                 send.at[:, pl.ds(0, cy), :],
                 target.at[pl.ds(1 + cx * ix, cx), 0, pl.ds(1 + cy * iy, cy), :],
@@ -604,10 +633,12 @@
                 in_sem,
                 (jx, jy, iz),
             ).start()
+
+    def far_start_sides(edge, side_target, in_sem):
         for side, dz in ((0, 1), (1, -1)):
             @when(z_there[dz])
             def _():
-                for jx, jy in column(False):
+                for jx, jy in reversed(list(column(False))):
                     remote(
                         edge.at[side, pl.ds(0, cy), :],
                         side_target.at[side, ix, pl.ds(cy * iy, cy), :],
@@ -663,25 +694,38 @@
             def _():
                 pl.semaphore_wait(chain.at[which], 1)
 
-    pass_on(1)
-    z_start(z_send, z_got, z_sem)
+    z_start(z_send, z_passed, z_sem)
     near_start(k_raw, k_raw, deep, True, near_sem.at[0])
     near_start(k_raw, k_raw, deep, False, near_sem.at[0])
+    pass_on(1)
+    coarse_edge(coarse_block(lambda p: k_raw[p, 0:2, own_rows, :], k_send), k_edge)
+    keep_own(k_send, k_mid)
+    z_pass_on(z_passed, z_got, z_sem)
     near_start(r_near, fine.r, deep - 1, False, near_sem.at[1])
     near_start(r_near, fine.r, deep - 1, True, near_sem.at[2])
-    coarse_block(lambda p: k_raw[p, 0:2, own_rows, :], k_send, k_edge)
-    keep_own(k_send, k_mid)
     for step in range(1, ny - 1):
         pass_wait(step)
         if step + 1 < ny - 1:
             pass_on(step + 1)
-    far_start(k_send, k_edge, k_mid, k_side, far_sem.at[0])
+    for side, dz in ((0, 1), (1, -1)):
+        @pl.when(z_there[dz])
+        def _():
+            pl.semaphore_signal(
+                chain.at[2 + side], inc=1, device_id=(ix, iy, iz + dz), device_id_type=MESH
+            )
 
     near_wait(deep, (True, False), near_sem.at[0])
-    z_wait(z_sem, False)
-    unpack_z(z_got, 0, k_raw, deep)
+    for side, dz in ((0, 1), (1, -1)):
+        @pl.when(z_there[-dz])
+        def _():
+            pl.semaphore_wait(chain.at[2 + side], 1)
+
+    far_start(k_send, k_mid, far_sem.at[0])
+    far_start_sides(k_edge, k_side, far_sem.at[0])
+    z_wait(z_passed, z_sem, False)
+    unpack_z(z_passed, z_got, 0, k_raw)
     fine.diagonal(k_raw, span(4), both)
-    unpack_z(z_got, 1, fine.r, deep)
+    unpack_z(z_passed, z_got, 1, fine.r)
     near_wait(deep - 1, (False,), near_sem.at[1])
 
     def strip(first, last):
@@ -693,31 +737,31 @@
             value = ref[own + q, 0:2, own_rows, :]
             x_fine[q] = value if fresh else x_fine[q] + value
 
-    def smooth_fine(first, last, grow):
+    def smooth_fine(first, last, grow, added):
         for number in range(DEGREE):
             pair = weights[number] if number < DEGREE - 1 else None
             rows, tiles = (both, None) if number < DEGREE - 1 else (middle, 2)
             fine.apply(strip(first, last), rows, pair, tiles)
-            if pair is not None:
+            if pair is not None and number < added:
                 add_fine(fine.now[0], max(first, 0), min(last, bx - 1))
             first, last = first + 1, last + grow
 
     centre, weights = chebyshev_coefs(DEGREE, smooth_low)
-    fine.first_update(strip(0, bx - 1), both, centre)
+    near_wait(deep - 1, (True,), near_sem.at[2])
+    fine.first_update(strip(-DEGREE, bx - 1), both, centre)
     add_fine(fine.now[0], fresh=True)
-    smooth_fine(1, bx - 1, 0)
-    near_wait(deep - 1, (True,), near_sem.at[2])
-    fine.first_update(strip(-DEGREE, -1), both, centre)
-    smooth_fine(1 - DEGREE, 0, 1)
-
+    smooth_fine(1 - DEGREE, bx - 1, 0, DEGREE)
+
+    far_wait(far_sem.at[0], True)
+    parts = coarse_block(residual_of, b_send)
+    far_start(b_send, mid.r, far_sem.at[1])
+    coarse_edge(parts, b_edge)
+    far_start_sides(b_edge, b_side, far_sem.at[1])
     near_sent((deep, deep - 1))
-    z_wait(z_sem, True)
-    coarse_block(residual_of, b_send, b_edge)
-    far_wait(far_sem.at[0], True)
-    far_start(b_send, b_edge, mid.r, b_side, far_sem.at[1])
+    z_wait(z_passed, z_sem, True)
     keep_own(b_send, mid.r)
     save_z(pack_z(fine.r, 0, None), zr_send)
-    z_start(zr_send, zr_got, zr_sem)
+    z_start(zr_send, zr_passed, zr_sem)
     near_start(fine.r, r_near, deep - 1, True, near_sem.at[3])
     near_start(fine.r, r_near, deep - 1, False, near_sem.at[3])
     own_fine = [(q, own + q) for q in range(bx)]
@@ -747,6 +791,7 @@
     to_low(lambda p, rows: k_mid[p, :, rows, :], k_low)
     low.diagonal(k_low, low_span, low_rows)
 
+    z_pass_on(zr_passed, zr_got, zr_sem)
     far_wait(far_sem.at[1])
     unpack_far(b_side, mid.r)
     start = 8
@@ -768,7 +813,10 @@
 
     to_low(lambda p, rows: mid.r[p, :, rows, :] * mid.dg[p, :, rows, :], low.r)
     low_centre, low_weights = chebyshev_coefs(COARSE_DEGREE, coarse_low)
+    near_wait(deep - 1, (True, False), near_sem.at[3])
+    z_wait(zr_passed, zr_sem, False)
     low.first_update(low_span, low_rows, low_centre)
+    unpack_z(zr_passed, zr_got, 0, r_near)
 
     def low_now():
         return low.now[0][1 : 1 + lows, 0, 1 : 1 + low_row, :]
@@ -796,9 +844,6 @@
         mid.apply(mid_span, mid_rows, pair)
         add_mid(mid.now[0])
 
-    near_wait(deep - 1, (True, False), near_sem.at[3])
-    z_wait(zr_sem, False)
-    unpack_z(zr_got, 0, r_near, deep)
     shape = (256, 384)
     from_lane, to_lane = cells(shape, 0), cells(shape, 1)
     to_lane = jnp.where(
@@ -826,13 +871,16 @@
     fine.r = r_near
     fine.apply(span(4), both, (0.0, 1.0 / centre))
     add_fine(fine.now[0])
-    smooth_fine(1 - DEGREE, bx - 1, 0)
+    smooth_fine(1 - DEGREE, bx - 1, 0, DEGREE - 2)
     for q, p in own_fine:
+        last, left = fine.new[0][p, 0:2, own_rows, :], residual_of(p)
         for t in range(2):
-            x_out[q, :, 128 * t : 128 * t + 128] = x_fine[q, t]
-            r_out[q, :, 128 * t : 128 * t + 128] = residual_of(p)[t]
+            at = (q, slice(None), slice(128 * t, 128 * t + 128))
+            x_out[at] = x_fine[q, t]
+            d_out[at] = last[t]
+            r_out[at] = left[t] - last[t]
     near_sent((deep - 1,))
-    z_wait(zr_sem, True)
+    z_wait(zr_passed, zr_sem, True)
     far_wait(far_sem.at[1], True)
 
 
@@ -840,7 +888,7 @@
     (nx, ny, nz) = sizes
     (bx, by, bz) = conductivity.shape
     kept = lambda *shape: pltpu.VMEM(shape, jnp.float32)
-    fine = kept(bx + 7, 3, 4 * by, 128)
+    fine = kept(bx + 7, 3, 3 * by, 128)
     mid = kept(nx * bx // 2 + 2, 2, ny * by // 2 + 8, 128)
     low = kept(nx * bx // 4 + 2, 1, ny * by // 4 + 8, 128)
     cx, cy = bx // 2, by // 2
@@ -849,23 +897,24 @@
     scratch += [kept(nx * cx // 2, ny * cy // 2, 128), kept(cx, 2, 2 * by, 128)]
     scratch += [kept(cx, by, 128)] * 2 + [kept(2, 2 * by, 128)] * 2
     scratch += [kept(2, nx, ny * cy, 128)] * 2
-    scratch += [kept(2, 2, by, 128), kept(2, 3, 2, by, 128)] * 2
+    scratch += [kept(2, 2, by, 128), kept(2, 2, by, 128), kept(2, 3, 2, by, 128)] * 2
     dma = pltpu.SemaphoreType.DMA
-    scratch += [dma((3,)), dma((3,)), dma((4,)), dma((2,)), dma((2,)), dma((1,)), dma((2,))]
-    scratch += [pltpu.SemaphoreType.REGULAR((2,))]
+    scratch += [dma((3,)), dma((5,)), dma((4,)), dma((4,)), dma((4,)), dma((1,)), dma((2,))]
+    scratch += [pltpu.SemaphoreType.REGULAR((4,))]
     shape = pltpu.VMEM((bx, by, bz), jnp.float32)
     vmem = pl.BlockSpec(memory_space=pltpu.VMEM)
     anywhere = pl.BlockSpec(memory_space=pltpu.HBM)
-    return pl.pallas_call(
+    x_part, r_part, last = pl.pallas_call(
         functools.partial(kernel, sizes, (bx, by, bz)),
-        out_shape=(shape, shape),
+        out_shape=(shape,) * 3,
         in_specs=[anywhere, anywhere],
-        out_specs=(vmem, vmem),
+        out_specs=(vmem,) * 3,
         scratch_shapes=scratch,
         compiler_params=pltpu.CompilerParams(
-            collective_id=0, has_side_effects=True, vmem_limit_bytes=66879488
+            collective_id=0, has_side_effects=True, vmem_limit_bytes=66715648
         ),
     )(conductivity, source)
+    return x_part + last, r_part + last
 
 
 def plan(conductivity, source):

time: 25.3 us -> 24.2 us (0.957)
  local copies, waits for them, and re-layouts: 1.26 us -> 0 us
  other arithmetic: 0 us -> 0.67 us
  Pallas kernels: 23.2 us -> 22.7 us
    unnamed x2 -> x0, local copies, waits for them, and re-layouts: 1.26 us -> none
    add x0 -> x1, other arithmetic: none -> 0.67 us  [gathered(): return (x_part + last, r_part + last)]
    pallas_call x1, Pallas kernels: 23.2 us -> 22.7 us  [gathered(): pl.pallas_call(functools.partial(kernel, sizes, (bx, by, bz)), out_shape=...]
where the time goes in v4:
time: 24.2 us; the launch traced here: 24 us
  Pallas kernels  22.7 us (94%)
  other arithmetic  0.67 us (3%)
  between operations  0.64 us (3%)
    pallas_call x1, Pallas kernels, gathered(): pl.pallas_call(functools.partial(kernel, sizes, (bx, by, bz)), out_shape=...  22.7 us
    add x1, other arithmetic, gathered(): return (x_part + last, r_part + last)  0.67 us

profile of v4, /device:TPU:1, one launch (start us, length us, event | category | flops | bytes accessed | tf_op | source)
XLA Modules:
  0.0 24.0 jit_solution(4131906517120700992)
XLA Ops:
  0.6 22.7 %shard_map.41 = (f32[8,8,256]{2,1,0:T(8,128)S(1)}, f32[8,8,256]{2,1,0:T(8,128)S(1)}, f32[8,8,256]{2,1,0:T(8,128)S(1)}) custom-call(f32[8,8,256]{2,1,0:T(8,128)} %refs_0_.1, f32[8,8,256]{2,1,0:T(8,128)} %refs_1_.1), custom_call_target="tpu_custom_call" | custom-call | tf_op jit(solution)/shard_map/pallas_call | solution.py:907
  23.4 0.7 %fusion = (f32[8,8,256]{2,1,0:T(8,128)}, f32[8,8,256]{2,1,0:T(8,128)}) fusion(f32[8,8,256]{2,1,0:T(8,128)S(1)} %get-tuple-element.7, f32[8,8,256]{2,1,0:T(8,128)S(1)} %get-tuple-element.6, f32[8,8,256]{2,1,0:T(8,128)S(1)} %get-tuple-element.5), kind=kLoop, calls=%fused_computation | loop fusion | flops 32768 | bytes 327680 | tf_op jit(solution)/shard_map/add | solution.py:917
